TPU v7x, 128 devices: a whole 4x4x4 slice. The times are simulated.
128 devices in a mesh: tok: 8 (over x_lo, z), feat: 16 (over y, x_hi, core).
Axes of the slice: x: 4 (x_hi: 2, x_lo: 2; x = x_hi * 2 + x_lo), y: 4, z: 4, core: 2. Of those that a mesh axis runs over, the one named last changes fastest.
Arguments:
- tokens_in: float32 [4096, 16384], P('tok', 'feat'), may hold values from -6 to 6
- key_weight: float32 [16384, 1024], P('feat'), may hold values from -0.046875 to 0.046875
- value_weight: float32 [16384, 1024], P('feat'), may hold values from -0.046875 to 0.046875
- blocks: float32 [4, 64, 256, 256], P(None, 'feat'), may hold values from -0.25 to 1.25, as said below
- row_order: int32 [4, 128], replicated, may hold values from 0 to 127, each once within a row
- key_grad: float32 [4096, 1024], P('tok', 'feat'), may hold values from -0.3 to 0.3
- value_grad: float32 [4096, 1024], P('tok', 'feat'), may hold values from -0.3 to 0.3
- moment: float32 [4, 64, 256, 256], P(None, 'feat', 'tok'), may hold values from -1.8 to 1.8
- second_moment: float32 [4, 64, 256, 256], P(None, 'feat', 'tok'), may hold values from 0.05 to 1
Outputs:
- key_out: float32 [4096, 1024], P('tok', 'feat')
- value_out: float32 [4096, 1024], P('tok', 'feat')
- new_blocks: float32 [4, 64, 256, 256], P(None, 'feat', 'tok')
- new_moment: float32 [4, 64, 256, 256], P(None, 'feat', 'tok')
- new_second: float32 [4, 64, 256, 256], P(None, 'feat', 'tok')
Inputs may be any that keep to these rules, and one draw needn't show every extreme that they name: `blocks`: every block is a dense 2 * 128 x 2 * 128 matrix. Each row of row_order is a permutation.
All inputs are finite; a program needn't handle non-finite values.
Results may differ from a plain program's by a relative error of at most 0.0001.
Values sent between devices are 32-bit elements; how exact they have to be, the bound alone decides.
A program may use at most 128 MiB of HBM per device.

v0:
```python
import jax
import jax.numpy as jnp
from jax import lax
from jax.experimental import pallas as pl
from jax.experimental.pallas import tpu as pltpu
from jax.sharding import PartitionSpec as P

MESH = pl.DeviceIdType.MESH
F32 = jnp.float32
BF16 = jnp.bfloat16
beta_one = 0.9
beta_two = 0.95
learn_rate = 0.01
epsilon = 1e-08
bias_one = 1.0 - 0.9**10
bias_two = 1.0 - 0.95**10

CT = 128
NC = 4
HT = 256


def split(v):
    hi = v.astype(BF16)
    lo = (v - hi.astype(F32)).astype(BF16)
    return hi, lo


def dims(ca, cb):
    return (((ca,), (cb,)), ((), ()))


def dot3(ah, al, bh, bl, ca=1, cb=0):
    d = dims(ca, cb)
    out = lax.dot_general(ah, bh, d, preferred_element_type=F32)
    out = out + lax.dot_general(ah, bl, d, preferred_element_type=F32)
    return out + lax.dot_general(al, bh, d, preferred_element_type=F32)


def kernel(
    x, kw, vw, bl, ro, kv, mo, se,
    ko, vo, nb, nm, ns,
    XP, WH, WL, AH, AL, TT, TS, ST, BS, R, I, T, G, J, GKV, KT, KP, LH, LL, YL, XL, FT, GO, GL, XG, AD,
    bsem, xsem, stsem, ktsem, adsem, osem,
    ss, rs, kvs, kvr, gs, gr, ps, pr, zs, zr, us, ur,
):
    tok = lax.axis_index("tok")
    feat = lax.axis_index("feat")
    z = lax.rem(tok, 4)
    xlo = lax.div(tok, 4)
    core = lax.rem(feat, 2)
    xhi = lax.rem(lax.div(feat, 2), 2)
    y = lax.div(feat, 4)
    yhi = lax.div(feat, 8)
    yx = lax.rem(feat, 4)
    chip = lax.div(feat, 2)
    bits = [None, core, xhi, yhi]
    steps = [None, 1, 2, 8]

    def flip(m):
        return (tok, feat + steps[m] - 2 * steps[m] * bits[m])

    core_peer, x_peer = flip(1), flip(2)

    def y_peer(d):
        return (tok, lax.rem(y + d, 4) * 4 + yx)

    def z_peer(d):
        return (xlo * 4 + lax.rem(z + d, 4), feat)

    xlo_peer = (lax.rem(tok + 4, 8), feat)

    def local_copy(src, dst, sem):
        return pltpu.make_async_copy(src, dst, sem)

    def remote(src, dst, s, r, dev):
        return pltpu.make_async_remote_copy(
            src_ref=src, dst_ref=dst, send_sem=s, recv_sem=r, device_id=dev, device_id_type=MESH
        )

    def rows(k, n=CT):
        return pl.ds(pl.multiple_of(k * n, n), n)

    def block_loads(m, slot):
        copies = []
        for i in range(2):
            for j in range(2):
                if m == 0:
                    r0, c0 = i * 128, j * 128
                else:
                    r0 = pl.multiple_of(lax.rem(bits[m] + i, 2) * 128, 128)
                    c0 = pl.multiple_of(lax.rem(bits[m] + j, 2) * 128, 128)
                copies.append(
                    local_copy(
                        bl.at[m, :, pl.ds(r0, 128), pl.ds(c0, 128)],
                        BS.at[pl.ds(4 * slot, 4), 2 * i + j],
                        bsem.at[m, 2 * i + j],
                    )
                )
        return copies

    def x_loads(k, to, at, sem):
        return [
            local_copy(x.at[pl.ds(k * CT, CT), pl.ds(h * 128, 128)], to(k, h), xsem.at[sem, k, h])
            for h in range(8)
        ]

    kt_load = local_copy(kv, KT, ktsem)
    kt_load.start()
    first_blocks = block_loads(0, 0)
    for cp in first_blocks:
        cp.start()
    x_copies = [x_loads(k, lambda k, h: XP.at[k // 2, k % 2, h], None, 0) for k in range(NC)]
    for cp in x_copies[0]:
        cp.start()
    second_blocks = block_loads(1, 1)
    for cp in second_blocks:
        cp.start()
    for k in range(1, NC):
        for cp in x_copies[k]:
            cp.start()

    def w_load(step):
        src = kw if step < 8 else vw
        return local_copy(src.at[pl.ds((step % 8) * 128, 128), :], ST.at[step % 2], stsem.at[step % 2])

    w_load(0).start()
    w_load(1).start()

    barrier = pltpu.get_barrier_semaphore()
    peers = [core_peer, x_peer, y_peer(1), y_peer(2), y_peer(3), z_peer(1), z_peer(2), z_peer(3), xlo_peer]
    for dev in peers:
        pl.semaphore_signal(barrier, inc=1, device_id=dev, device_id_type=MESH)

    for m in range(4):
        order = jnp.broadcast_to(ro[m : m + 1, :], (128, 128))
        hot = (lax.broadcasted_iota(jnp.int32, (128, 128), 0) == order).astype(F32)
        TT[m] = hot.astype(BF16)
        TS[m] = jnp.transpose(hot).astype(BF16)

    def prepare(m, slot, copies):
        for cp in copies:
            cp.wait()
        table = TS[m]

        def one(c, carry):
            for i in range(2):
                for j in range(2):
                    hi, lo = split(BS[4 * slot + c, 2 * i + j])
                    ph = jnp.dot(table, hi, preferred_element_type=F32)
                    p_lo = jnp.dot(table, lo, preferred_element_type=F32)
                    AH[m, c, i * 128 : (i + 1) * 128, j * 128 : (j + 1) * 128] = ph.astype(BF16)
                    AL[m, c, i * 128 : (i + 1) * 128, j * 128 : (j + 1) * 128] = p_lo.astype(BF16)
            return carry

        lax.fori_loop(0, 4, one, 0)

    prepare(0, 0, first_blocks)
    third_blocks = block_loads(2, 0)
    for cp in third_blocks:
        cp.start()

    pl.semaphore_wait(barrier, len(peers))

    def fwd_out(m, k):
        return remote(
            R.at[m - 1, 1 - bits[m], :, rows(k)], I.at[m - 1, :, rows(k)],
            ss.at[0, m - 1, 0, k], rs.at[0, m - 1, 0, k], flip(m),
        )

    def fwd_back(m, k):
        return remote(
            T.at[m - 1, :, rows(k)], R.at[m, bits[m], :, rows(k)],
            ss.at[0, m - 1, 1, k], rs.at[0, m - 1, 1, k], flip(m),
        )

    def bwd_out(m, k):
        return remote(
            G.at[m, 1 - bits[m], :, rows(k)], J.at[m - 1, :, rows(k)],
            ss.at[1, m - 1, 0, k], rs.at[1, m - 1, 0, k], flip(m),
        )

    def bwd_back(m, k):
        return remote(
            T.at[m - 1, :, rows(k)], G.at[m - 1, bits[m], :, rows(k)],
            ss.at[1, m - 1, 1, k], rs.at[1, m - 1, 1, k], flip(m),
        )

    def first_factor(k):
        for cp in x_copies[k]:
            cp.wait()
        for u in range(2):
            for c in range(2):
                h = 4 * u + 2 * c
                pair = jnp.concatenate([XP[k // 2, k % 2, h], XP[k // 2, k % 2, h + 1]], axis=1)
                hi, lo = split(pair)
                out = dot3(hi, lo, AH[0, 2 * u + c], AL[0, 2 * u + c])
                R[0, u, 2 * c, k * CT : (k + 1) * CT] = out[:, :128]
                R[0, u, 2 * c + 1, k * CT : (k + 1) * CT] = out[:, 128:]

    def fwd_factor(m, k):
        own = bits[m]

        def one(c, carry):
            pair = jnp.concatenate([R[m - 1, own, c, rows(k)], I[m - 1, c, rows(k)]], axis=1)
            hi, lo = split(pair)
            out = dot3(hi, lo, AH[m, c], AL[m, c])
            R[m, own, c, rows(k)] = out[:, :128]
            T[m - 1, c, rows(k)] = out[:, 128:]
            return carry

        lax.fori_loop(0, 4, one, 0)

    def bwd_factor(m, k):
        own = bits[m]

        def one(c, carry):
            pair = jnp.concatenate([G[m, own, c, rows(k)], J[m - 1, c, rows(k)]], axis=1)
            hi, lo = split(pair)
            out = dot3(hi, lo, AH[m, c], AL[m, c], 1, 1)
            G[m - 1, own, c, rows(k)] = out[:, :128]
            T[m - 1, c, rows(k)] = out[:, 128:]
            return carry

        lax.fori_loop(0, 4, one, 0)

    kt_load.wait()
    pair_copy = remote(KT, KP, kvs.at[0], kvr.at[0], core_peer)
    pair_copy.start()

    for k in range(NC):
        first_factor(k)
        fwd_out(1, k).start()

    pair_copy.wait_recv()
    lane = lax.broadcasted_iota(jnp.int32, (512, 128), 1)
    mine = (lane < 64) == (core == 0)
    GKV[core, chip] = jnp.where(mine, KT[...], pltpu.roll(KP[...], 64, 1))

    def gx(h):
        return remote(
            GKV.at[core, chip, rows(h, HT)], GKV.at[core, chip, rows(h, HT)],
            kvs.at[1 + h], kvr.at[1 + h], x_peer,
        )

    chip_x = chip + 1 - 2 * xhi

    def gy(d, h, far):
        tile = chip_x if far else chip
        return remote(
            GKV.at[core, tile, rows(h, HT)], GKV.at[core, tile, rows(h, HT)],
            gs.at[far, d - 1, h], gr.at[far, d - 1, h], y_peer(d),
        )

    def gc(h):
        return remote(
            GKV.at[core, :, rows(h, HT)], GKV.at[core, :, rows(h, HT)],
            kvs.at[3 + h], kvr.at[3 + h], core_peer,
        )

    for h in range(2):
        gx(h).start()
    for h in range(2):
        for d in (1, 3, 2):
            gy(d, h, 0).start()

    prepare(1, 1, second_blocks)
    fourth_blocks = block_loads(3, 1)
    for cp in fourth_blocks:
        cp.start()

    for k in range(NC):
        fwd_out(1, k).wait_recv()
        fwd_factor(1, k)
        fwd_back(1, k).start()

    prepare(2, 0, third_blocks)

    for k in range(NC):
        fwd_back(1, k).wait_recv()
        fwd_out(2, k).start()

    for h in range(2):
        gx(h).wait_recv()
        for d in (1, 3, 2):
            gy(d, h, 1).start()

    prepare(3, 1, fourth_blocks)

    for step in range(16):
        w_load(step).wait()
        s, base = step // 8, (step % 8) * 128

        def strip(i, carry, s=s, base=base, slot=step % 2):
            hi, lo = split(ST[slot, pl.ds(pl.multiple_of(i * 32, 32), 32), :])
            at = pl.ds(pl.multiple_of(base + i * 32, 32), 32)
            for q in range(4):
                WH[s, q, at, :] = hi[:, q * 256 : (q + 1) * 256]
                WL[s, q, at, :] = lo[:, q * 256 : (q + 1) * 256]
            return carry

        lax.fori_loop(0, 4, strip, 0)
        if step + 2 < 16:
            w_load(step + 2).start()

    x_again = [x_loads(k, lambda k, h: BS.at[2 * k + h // 4, h % 4], None, 1) for k in range(NC)]
    for group in x_again:
        for cp in group:
            cp.start()
    share = pl.ds(pl.multiple_of(tok * 32, 32), 32)
    adam_loads = [
        local_copy(mo, AD.at[0], adsem.at[0]),
        local_copy(se, AD.at[1], adsem.at[1]),
        local_copy(bl.at[:, :, share, :], AD.at[2], adsem.at[2]),
    ]
    for cp in adam_loads:
        cp.start()

    def gathered(h):
        for far in range(2):
            for d in (1, 3, 2):
                gy(d, h, far).wait_recv()
        gc(h).start()

    def upstream(h):
        gc(h).wait_recv()
        for s in range(2):
            for t in range(8):
                hi, lo = split(GKV[s, t, h * HT : (h + 1) * HT, :])
                LH[s, :, t * 128 : (t + 1) * 128] = hi
                LL[s, :, t * 128 : (t + 1) * 128] = lo
        for u in range(2):

            def one(n, carry, u=u):
                at = pl.ds(pl.multiple_of(u * 512 + n * 256, 256), 256)
                acc = None
                for s in range(2):
                    for q in range(4):
                        lh = LH[s, :, q * 256 : (q + 1) * 256]
                        ll = LL[s, :, q * 256 : (q + 1) * 256]
                        part = dot3(lh, ll, WH[s, q, at, :], WL[s, q, at, :], 1, 1)
                        acc = part if acc is None else acc + part
                G[3, u, 2 * n, h * HT : (h + 1) * HT] = acc[:, :128]
                G[3, u, 2 * n + 1, h * HT : (h + 1) * HT] = acc[:, 128:]
                return carry

            lax.fori_loop(0, 2, one, 0)
        for k in (2 * h, 2 * h + 1):
            bwd_out(3, k).start()

    def fwd_step(m, k):
        fwd_out(m, k).wait_recv()
        fwd_factor(m, k)
        fwd_back(m, k).start()

    def bwd_step(m, k):
        bwd_out(m, k).wait_recv()
        bwd_factor(m, k)
        bwd_back(m, k).start()

    def fwd_next(m, k):
        fwd_back(m - 1, k).wait_recv()
        fwd_out(m, k).start()

    def bwd_next(m, k):
        bwd_back(m + 1, k).wait_recv()
        bwd_out(m, k).start()

    fwd_step(2, 0)
    gathered(0)
    fwd_step(2, 1)
    upstream(0)
    fwd_step(2, 2)
    gathered(1)
    fwd_step(2, 3)
    upstream(1)
    for k in range(NC):
        bwd_step(3, k)
    for k in range(NC):
        fwd_next(3, k)

    def gradient(m):
        own = 0 if m == 0 else bits[m]

        def one(c, carry):
            total = None
            for t in range(2):
                if m == 0:
                    left = jnp.concatenate(
                        [
                            jnp.concatenate(
                                [BS[2 * k + lax.div(c, 2), 2 * lax.rem(c, 2) + i] for i in range(2)], axis=1
                            )
                            for k in (2 * t, 2 * t + 1)
                        ],
                        axis=0,
                    )
                    u, base = lax.div(c, 2), 2 * lax.rem(c, 2)
                    right = jnp.concatenate([G[0, u, base + i, t * HT : (t + 1) * HT] for i in range(2)], axis=1)
                else:
                    at = slice(t * HT, (t + 1) * HT)
                    left = jnp.concatenate([R[m - 1, own, c, at], I[m - 1, c, at]], axis=1)
                    right = jnp.concatenate([G[m, own, c, at], J[m - 1, c, at]], axis=1)
                lh, ll = split(left)
                rh, rl = split(right)
                part = dot3(lh, ll, rh, rl, 0, 0)
                total = part if total is None else total + part
            table = TT[m]
            for i in range(2):
                hi, lo = split(total[i * 128 : (i + 1) * 128])
                back = jnp.dot(table, hi, preferred_element_type=F32) + jnp.dot(
                    table, lo, preferred_element_type=F32
                )
                ii = i if m == 0 else lax.rem(own + i, 2)
                for j in range(2):
                    jj = j if m == 0 else lax.rem(own + j, 2)
                    for zz in range(4):
                        GO[m, zz, ii, c, jj] = back[zz * 32 : (zz + 1) * 32, j * 128 : (j + 1) * 128]
            return carry

        lax.fori_loop(0, 4, one, 0)
        for d in (1, 3, 2):
            z_send(m, d).start()

    def z_send(m, d):
        return remote(
            GO.at[m, lax.rem(z + d, 4)], GL.at[m, d - 1], zs.at[m, d - 1], zr.at[m, d - 1], z_peer(d)
        )

    def u_send(m):
        return remote(GO.at[m, z, 1 - xlo], XG.at[m], us.at[m], ur.at[m], xlo_peer)

    def z_sum(m):
        for d in (1, 3, 2):
            z_send(m, d).wait_recv()
        for side in (1 - xlo, xlo):
            GO[m, z, side] = GO[m, z, side] + GL[m, 0, side] + GL[m, 1, side] + GL[m, 2, side]
        u_send(m).start()

    def adam(m):
        u_send(m).wait_recv()

        def one(c, carry):
            for j in range(2):
                at = slice(j * 128, (j + 1) * 128)
                grad = GO[m, z, xlo, c, j] + XG[m, c, j]
                moment = beta_one * AD[0, m, c, :, at] + (1.0 - beta_one) * grad
                second = beta_two * AD[1, m, c, :, at] + (1.0 - beta_two) * grad * grad
                step = learn_rate * (moment / bias_one) / (jnp.sqrt(second / bias_two) + epsilon)
                AD[0, m, c, :, at] = moment
                AD[1, m, c, :, at] = second
                AD[2, m, c, :, at] = AD[2, m, c, :, at] - step
            return carry

        lax.fori_loop(0, 4, one, 0)
        for i, out in enumerate((nm, ns, nb)):
            result(m, i, out).start()

    def result(m, i, out):
        return local_copy(AD.at[i, m], out.at[m], osem.at[i, m])

    def p_core(k):
        return remote(
            XP.at[k % 2, 1 - core], GKV.at[0, :, rows(k)], ps.at[0, k], pr.at[0, k], core_peer
        )

    def p_y(k, d):
        yy = lax.rem(y + d, 4)
        return remote(
            XP.at[k % 2, core, pl.ds(2 * yy, 2)], YL.at[d - 1, k], ps.at[d, k], pr.at[d, k], y_peer(d)
        )

    def p_x(k):
        return remote(
            XP.at[k % 2, core, 2 * y + 1 - xhi], XL.at[k], ps.at[4, k], pr.at[4, k], x_peer
        )

    def p_last(k):
        return remote(FT.at[k], KP.at[rows(k)], ps.at[5, k], pr.at[5, k], core_peer)

    def project(k):
        if k >= 2:
            p_core(k - 2).wait_send()
            for d in (1, 3, 2):
                p_y(k - 2, d).wait_send()
            p_x(k - 2).wait_send()
        for u in range(2):
            for c in range(4):
                hi, lo = split(R[3, u, c, k * CT : (k + 1) * CT])
                at = slice((u * 4 + c) * 128, (u * 4 + c + 1) * 128)
                LH[0, :CT, at] = hi
                LL[0, :CT, at] = lo
        for s in range(2):

            def one(n, carry, s=s):
                out = dot3(LH[0, :CT, :], LL[0, :CT, :], WH[s, n], WL[s, n])
                XP[k % 2, s, 2 * n] = out[:, :128]
                XP[k % 2, s, 2 * n + 1] = out[:, 128:]
                return carry

            lax.fori_loop(0, 4, one, 0)
        p_core(k).start()

    def project_y(k):
        p_core(k).wait_recv()

        def one(t, carry):
            XP[k % 2, core, t] = XP[k % 2, core, t] + GKV[0, t, k * CT : (k + 1) * CT]
            return carry

        lax.fori_loop(0, 8, one, 0)
        for d in (1, 3, 2):
            p_y(k, d).start()

    def project_x(k):
        for d in (1, 3, 2):
            p_y(k, d).wait_recv()
        for side in (1 - xhi, xhi):
            at = 2 * y + side
            XP[k % 2, core, at] = XP[k % 2, core, at] + YL[0, k, side] + YL[1, k, side] + YL[2, k, side]
        p_x(k).start()

    def project_last(k):
        p_x(k).wait_recv()
        FT[k] = XP[k % 2, core, 2 * y + xhi] + XL[k]
        p_last(k).start()

    def project_out(k):
        p_last(k).wait_recv()
        at = slice(k * CT, (k + 1) * CT)
        key_tile = jnp.where(core == 0, FT[k], KP[at])
        value_tile = jnp.where(core == 0, KP[at], FT[k])
        key_tile = jnp.where(core == 0, key_tile, pltpu.roll(key_tile, 64, 1))
        value_tile = jnp.where(core == 0, value_tile, pltpu.roll(value_tile, 64, 1))
        ko[at, :] = key_tile[:, :64]
        vo[at, :] = value_tile[:, :64]

    def fwd_last(k):
        bwd_back(3, k).wait_send()
        fwd_step(3, k)

    def bwd_mid(k):
        fwd_back(2, k).wait_send()
        bwd_step(2, k)

    def bwd_low(k):
        fwd_back(1, k).wait_send()
        bwd_step(1, k)

    bwd_next(2, 0)
    bwd_next(2, 1)
    bwd_mid(0)
    bwd_next(2, 2)
    bwd_mid(1)
    bwd_next(2, 3)
    bwd_mid(2)
    fwd_last(0)
    for h in range(2):
        gx(h).wait_send()
        gc(h).wait_send()
        for far in range(2):
            for d in (1, 3, 2):
                gy(d, h, far).wait_send()
    bwd_next(1, 0)
    bwd_mid(3)
    fwd_last(1)
    bwd_low(0)
    bwd_next(1, 1)
    fwd_last(2)
    bwd_low(1)
    bwd_next(1, 2)
    fwd_last(3)
    bwd_low(2)
    gradient(3)
    gradient(2)
    pair_copy.wait_send()
    fwd_back(3, 0).wait_recv()
    project(0)
    bwd_next(1, 3)
    project_y(0)
    bwd_low(3)
    fwd_back(3, 1).wait_recv()
    project(1)
    for k in range(NC):
        bwd_back(1, k).wait_recv()
    gradient(1)
    for group in x_again:
        for cp in group:
            cp.wait()
    gradient(0)
    project_y(1)
    project_x(0)
    project_last(0)
    for cp in adam_loads:
        cp.wait()
    project_x(1)
    project_last(1)
    fwd_back(3, 2).wait_recv()
    project(2)
    fwd_back(3, 3).wait_recv()
    project_y(2)
    z_sum(3)
    project(3)
    z_sum(2)
    project_y(3)
    project_out(0)
    project_out(1)
    adam(3)
    adam(2)
    z_sum(1)
    project_x(2)
    project_last(2)
    z_sum(0)
    project_x(3)
    project_last(3)
    adam(1)
    adam(0)
    project_out(2)
    project_out(3)

    for m in (1, 2, 3):
        for k in range(NC):
            fwd_out(m, k).wait_send()
            bwd_out(m, k).wait_send()
    for k in range(NC):
        fwd_back(3, k).wait_send()
        bwd_back(2, k).wait_send()
        bwd_back(1, k).wait_send()
        p_last(k).wait_send()
    for k in (2, 3):
        p_core(k).wait_send()
        for d in (1, 3, 2):
            p_y(k, d).wait_send()
        p_x(k).wait_send()
    for m in range(4):
        for d in (1, 3, 2):
            z_send(m, d).wait_send()
        u_send(m).wait_send()
        for i, out in enumerate((nm, ns, nb)):
            result(m, i, out).wait()


def local(x, kw, vw, bl, ro, kg, vg, mo, se):
    kv = jnp.concatenate([kg, vg], axis=1)
    hbm = pl.BlockSpec(memory_space=pl.ANY)
    vmem = pl.BlockSpec(memory_space=pltpu.VMEM)
    dma = pltpu.SemaphoreType.DMA
    tile = (128, 128)
    scratch = [
        pltpu.VMEM((2, 2, 8) + tile, F32),
        pltpu.VMEM((2, 4, 1024, 256), BF16),
        pltpu.VMEM((2, 4, 1024, 256), BF16),
        pltpu.VMEM((4, 4, 256, 256), BF16),
        pltpu.VMEM((4, 4, 256, 256), BF16),
        pltpu.VMEM((4,) + tile, BF16),
        pltpu.VMEM((4,) + tile, BF16),
        pltpu.VMEM((2, 128, 1024), F32),
        pltpu.VMEM((8, 4) + tile, F32),
        pltpu.VMEM((4, 2, 4, 512, 128), F32),
        pltpu.VMEM((3, 4, 512, 128), F32),
        pltpu.VMEM((3, 4, 512, 128), F32),
        pltpu.VMEM((4, 2, 4, 512, 128), F32),
        pltpu.VMEM((3, 4, 512, 128), F32),
        pltpu.VMEM((2, 8, 512, 128), F32),
        pltpu.VMEM((512, 128), F32),
        pltpu.VMEM((512, 128), F32),
        pltpu.VMEM((2, 256, 1024), BF16),
        pltpu.VMEM((2, 256, 1024), BF16),
        pltpu.VMEM((3, 4, 2) + tile, F32),
        pltpu.VMEM((4,) + tile, F32),
        pltpu.VMEM((4,) + tile, F32),
        pltpu.VMEM((4, 4, 2, 4, 2, 32, 128), F32),
        pltpu.VMEM((4, 3, 2, 4, 2, 32, 128), F32),
        pltpu.VMEM((4, 4, 2, 32, 128), F32),
        pltpu.VMEM((3, 4, 4, 32, 256), F32),
        dma((4, 4)),
        dma((2, 4, 8)),
        dma((2,)),
        dma(()),
        dma((3,)),
        dma((3, 4)),
        dma((2, 3, 2, 4)),
        dma((2, 3, 2, 4)),
        dma((5,)),
        dma((5,)),
        dma((2, 3, 2)),
        dma((2, 3, 2)),
        dma((6, 4)),
        dma((6, 4)),
        dma((4, 3)),
        dma((4, 3)),
        dma((4,)),
        dma((4,)),
    ]
    share = jax.ShapeDtypeStruct((4, 4, 32, 256), F32)
    narrow = jax.ShapeDtypeStruct((512, 64), F32)
    return pl.pallas_call(
        kernel,
        out_shape=(narrow, narrow, share, share, share),
        in_specs=[hbm, hbm, hbm, hbm, vmem, hbm, hbm, hbm],
        out_specs=(vmem, vmem, hbm, hbm, hbm),
        scratch_shapes=scratch,
        compiler_params=pltpu.CompilerParams(
            collective_id=0, has_side_effects=True, vmem_limit_bytes=67043328
        ),
    )(x, kw, vw, bl, ro, kv, mo, se)


def solution(mesh):
    placed = (
        P("tok", "feat"),
        P("feat", None),
        P("feat", None),
        P(None, "feat", None, None),
        P(),
        P("tok", "feat"),
        P("tok", "feat"),
        P(None, "feat", "tok", None),
        P(None, "feat", "tok", None),
    )
    return jax.shard_map(
        local,
        mesh=mesh,
        in_specs=placed,
        out_specs=(
            P("tok", "feat"),
            P("tok", "feat"),
            P(None, "feat", "tok", None),
            P(None, "feat", "tok", None),
            P(None, "feat", "tok", None),
        ),
        check_vma=False,
    )
```

profile of v0, /device:TPU:1, one launch (start us, length us, event | category | flops | bytes accessed | tf_op | source)
XLA Modules:
  0.0 188.1 jit_solution(8986157226710862941)
XLA Ops:
  0.6 1.0 copy.14
  1.7 1.0 copy.15
  2.7 0.8 pad_maximum_fusion.kv
  3.5 175.5 %shard_map.128 = (f32[512,64]{1,0:T(8,128)}, f32[512,64]{1,0:T(8,128)}, f32[4,4,32,256]{3,2,1,0:T(8,128)}, f32[4,4,32,256]{3,2,1,0:T(8,128)}, f32[4,4,32,256]{3,2,1,0:T(8,128)}) custom-call(f32[512,1024]{1,0:T(8,128)} %x.1, f32[1024,1024]{1,0:T(8,128)} %kw.1, f32[1024,1024]{1,0:T(8,128)} %vw.1, f32[4,4,256,256]{3,2,1,0:T(8,128)} %bl.1, s32[4,128]{1,0:T(4,128)} %ro.1, ...), custom_call_target="tpu_custom_call" | custom-call | tf_op jit(solution)/shard_map/pallas_call | solution.py:697
  179.0 1.7 copy.16
  180.7 1.7 copy.17
  182.5 1.9 copy.21
  184.3 1.9 copy.22
  186.2 1.9 copy.23
where the time goes:
time: 189 us; the launch traced here: 188 us
  Pallas kernels  175 us (93%)
  local copies, waits for them, and re-layouts  11.1 us (6%)
    pallas_call x1, Pallas kernels, local(): pl.pallas_call(kernel, out_shape=(narrow, narrow, share, share, share), i...  175 us
    unnamed x5, local copies, waits for them, and re-layouts  7.7 us

commit v1 on v0

--- a/solution.py
+++ b/solution.py
@@ -15,6 +15,21 @@
 bias_one = 1.0 - 0.9**10
 bias_two = 1.0 - 0.95**10
 
+ORDER = (
+    ("W", 0), ("W", 1), ("T",), ("TY", 0), ("B", 1), ("B", 2), ("B", 0), ("C", 1), ("B", 3),
+    ("W", 2), ("W", 3), ("C", 0), ("C", 3), ("X", 0), ("TY", 1), ("Q", 2), ("W", 4), ("W", 5),
+    ("D", 1), ("Z", 0), ("W", 6), ("W", 7), ("X", 1), ("H", 0), ("HS", 0), ("Q", 3), ("Z", 1),
+    ("HS", 1), ("D", 3), ("D", 0), ("I", 0), ("H", 1), ("I", 1), ("C", 2), ("HS", 3), ("J", 0),
+    ("HS", 2), ("J", 1), ("K", 0), ("I", 3), ("K", 1), ("I", 2), ("G", 2, 0), ("L", 0), ("E", 1),
+    ("E", 0), ("J", 3), ("M", 0), ("L", 1), ("J", 2), ("M", 1), ("G", 1, 0), ("K", 3), ("F", 1),
+    ("D", 2), ("N", 0), ("K", 2), ("F", 0), ("E", 3), ("G", 2, 1), ("G", 3, 0), ("L", 3), ("P", 1),
+    ("M", 3), ("PY", 1), ("P", 0), ("E", 2), ("L", 2), ("PY", 0), ("F", 3), ("S", 2), ("M", 2),
+    ("G", 1, 1), ("N", 1), ("PX", 1), ("U", 2), ("F", 2), ("G", 3, 1), ("PX", 0), ("S", 1),
+    ("SX",), ("PL", 1), ("P", 3), ("U", 1), ("PY", 3), ("PL", 0), ("P", 2), ("S", 3), ("PO", 1),
+    ("PO", 0), ("PY", 2), ("U", 0), ("PX", 3), ("U", 3), ("PL", 3), ("PX", 2), ("PO", 3),
+    ("PL", 2), ("PO", 2),
+)
+
 CT = 128
 NC = 4
 HT = 256
@@ -38,10 +53,10 @@
 
 
 def kernel(
-    x, kw, vw, bl, ro, kv, mo, se,
-    ko, vo, nb, nm, ns,
-    XP, WH, WL, AH, AL, TT, TS, ST, BS, R, I, T, G, J, GKV, KT, KP, LH, LL, YL, XL, FT, GO, GL, XG, AD,
-    bsem, xsem, stsem, ktsem, adsem, osem,
+    x, kw, vw, bl, ro, kg, vg,
+    go, kvo,
+    XP, WH, WL, AH, AL, TT, TS, ST, BS, R, I, T, G, J, GKV, KT, KP, LH, LL, YL, XL, FT, GO, GL, XG, KV,
+    bsem, xsem, stsem, ktsem, osem,
     ss, rs, kvs, kvr, gs, gr, ps, pr, zs, zr, us, ur,
 ):
     tok = lax.axis_index("tok")
@@ -105,8 +120,12 @@
             for h in range(8)
         ]
 
-    kt_load = local_copy(kv, KT, ktsem)
-    kt_load.start()
+    kt_loads = [
+        local_copy(kg, KV.at[pl.ds(0, 64)], ktsem.at[0]),
+        local_copy(vg, KV.at[pl.ds(64, 64)], ktsem.at[1]),
+    ]
+    for cp in kt_loads:
+        cp.start()
     first_blocks = block_loads(0, 0)
     for cp in first_blocks:
         cp.start()
@@ -122,10 +141,10 @@
 
     def w_load(step):
         src = kw if step < 8 else vw
-        return local_copy(src.at[pl.ds((step % 8) * 128, 128), :], ST.at[step % 2], stsem.at[step % 2])
-
-    w_load(0).start()
-    w_load(1).start()
+        return local_copy(src.at[pl.ds((step % 8) * 128, 128), :], ST.at[step % 4], stsem.at[step % 4])
+
+    for step in range(4):
+        w_load(step).start()
 
     barrier = pltpu.get_barrier_semaphore()
     peers = [core_peer, x_peer, y_peer(1), y_peer(2), y_peer(3), z_peer(1), z_peer(2), z_peer(3), xlo_peer]
@@ -159,8 +178,6 @@
     third_blocks = block_loads(2, 0)
     for cp in third_blocks:
         cp.start()
-
-    pl.semaphore_wait(barrier, len(peers))
 
     def fwd_out(m, k):
         return remote(
@@ -224,18 +241,8 @@
 
         lax.fori_loop(0, 4, one, 0)
 
-    kt_load.wait()
     pair_copy = remote(KT, KP, kvs.at[0], kvr.at[0], core_peer)
-    pair_copy.start()
-
-    for k in range(NC):
-        first_factor(k)
-        fwd_out(1, k).start()
-
-    pair_copy.wait_recv()
-    lane = lax.broadcasted_iota(jnp.int32, (512, 128), 1)
-    mine = (lane < 64) == (core == 0)
-    GKV[core, chip] = jnp.where(mine, KT[...], pltpu.roll(KP[...], 64, 1))
+    chip_x = chip + 1 - 2 * xhi
 
     def gx(h):
         return remote(
@@ -243,8 +250,6 @@
             kvs.at[1 + h], kvr.at[1 + h], x_peer,
         )
 
-    chip_x = chip + 1 - 2 * xhi
-
     def gy(d, h, far):
         tile = chip_x if far else chip
         return remote(
@@ -258,63 +263,51 @@
             kvs.at[3 + h], kvr.at[3 + h], core_peer,
         )
 
-    for h in range(2):
-        gx(h).start()
-    for h in range(2):
+    def tiles_send():
+        for cp in kt_loads:
+            cp.wait()
+        KT[...] = jnp.transpose(KV[...])
+
+    def tiles():
+        pair_copy.wait_recv()
+        lane = lax.broadcasted_iota(jnp.int32, (512, 128), 1)
+        mine = (lane < 64) == (core == 0)
+        GKV[core, chip] = jnp.where(mine, KT[...], pltpu.roll(KP[...], 64, 1))
+        for h in range(2):
+            gx(h).start()
+
+    def gather_near(h):
         for d in (1, 3, 2):
             gy(d, h, 0).start()
 
-    prepare(1, 1, second_blocks)
-    fourth_blocks = block_loads(3, 1)
-    for cp in fourth_blocks:
-        cp.start()
-
-    for k in range(NC):
+    def gather_far(h):
+        gx(h).wait_recv()
+        for d in (1, 3, 2):
+            gy(d, h, 1).start()
+
+    def fwd_first(k):
         fwd_out(1, k).wait_recv()
         fwd_factor(1, k)
         fwd_back(1, k).start()
 
-    prepare(2, 0, third_blocks)
-
-    for k in range(NC):
-        fwd_back(1, k).wait_recv()
-        fwd_out(2, k).start()
-
-    for h in range(2):
-        gx(h).wait_recv()
-        for d in (1, 3, 2):
-            gy(d, h, 1).start()
-
-    prepare(3, 1, fourth_blocks)
-
-    for step in range(16):
-        w_load(step).wait()
-        s, base = step // 8, (step % 8) * 128
-
-        def strip(i, carry, s=s, base=base, slot=step % 2):
-            hi, lo = split(ST[slot, pl.ds(pl.multiple_of(i * 32, 32), 32), :])
-            at = pl.ds(pl.multiple_of(base + i * 32, 32), 32)
-            for q in range(4):
-                WH[s, q, at, :] = hi[:, q * 256 : (q + 1) * 256]
-                WL[s, q, at, :] = lo[:, q * 256 : (q + 1) * 256]
-            return carry
-
-        lax.fori_loop(0, 4, strip, 0)
-        if step + 2 < 16:
-            w_load(step + 2).start()
+    def weights(part):
+        for step in range(2 * part, 2 * part + 2):
+            w_load(step).wait()
+            s, base = step // 8, (step % 8) * 128
+
+            def strip(i, carry, s=s, base=base, slot=step % 4):
+                hi, lo = split(ST[slot, pl.ds(pl.multiple_of(i * 32, 32), 32), :])
+                at = pl.ds(pl.multiple_of(base + i * 32, 32), 32)
+                for q in range(4):
+                    WH[s, q, at, :] = hi[:, q * 256 : (q + 1) * 256]
+                    WL[s, q, at, :] = lo[:, q * 256 : (q + 1) * 256]
+                return carry
+
+            lax.fori_loop(0, 4, strip, 0)
+            if step + 4 < 16:
+                w_load(step + 4).start()
 
     x_again = [x_loads(k, lambda k, h: BS.at[2 * k + h // 4, h % 4], None, 1) for k in range(NC)]
-    for group in x_again:
-        for cp in group:
-            cp.start()
-    share = pl.ds(pl.multiple_of(tok * 32, 32), 32)
-    adam_loads = [
-        local_copy(mo, AD.at[0], adsem.at[0]),
-        local_copy(se, AD.at[1], adsem.at[1]),
-        local_copy(bl.at[:, :, share, :], AD.at[2], adsem.at[2]),
-    ]
-    for cp in adam_loads:
-        cp.start()
 
     def gathered(h):
         for far in range(2):
@@ -345,8 +338,6 @@
                 return carry
 
             lax.fori_loop(0, 2, one, 0)
-        for k in (2 * h, 2 * h + 1):
-            bwd_out(3, k).start()
 
     def fwd_step(m, k):
         fwd_out(m, k).wait_recv()
@@ -366,45 +357,29 @@
         bwd_back(m + 1, k).wait_recv()
         bwd_out(m, k).start()
 
-    fwd_step(2, 0)
-    gathered(0)
-    fwd_step(2, 1)
-    upstream(0)
-    fwd_step(2, 2)
-    gathered(1)
-    fwd_step(2, 3)
-    upstream(1)
-    for k in range(NC):
-        bwd_step(3, k)
-    for k in range(NC):
-        fwd_next(3, k)
-
-    def gradient(m):
+    def gradient(m, t):
         own = 0 if m == 0 else bits[m]
 
         def one(c, carry):
-            total = None
-            for t in range(2):
-                if m == 0:
-                    left = jnp.concatenate(
-                        [
-                            jnp.concatenate(
-                                [BS[2 * k + lax.div(c, 2), 2 * lax.rem(c, 2) + i] for i in range(2)], axis=1
-                            )
-                            for k in (2 * t, 2 * t + 1)
-                        ],
-                        axis=0,
-                    )
-                    u, base = lax.div(c, 2), 2 * lax.rem(c, 2)
-                    right = jnp.concatenate([G[0, u, base + i, t * HT : (t + 1) * HT] for i in range(2)], axis=1)
-                else:
-                    at = slice(t * HT, (t + 1) * HT)
-                    left = jnp.concatenate([R[m - 1, own, c, at], I[m - 1, c, at]], axis=1)
-                    right = jnp.concatenate([G[m, own, c, at], J[m - 1, c, at]], axis=1)
-                lh, ll = split(left)
-                rh, rl = split(right)
-                part = dot3(lh, ll, rh, rl, 0, 0)
-                total = part if total is None else total + part
+            if m == 0:
+                left = jnp.concatenate(
+                    [
+                        jnp.concatenate(
+                            [BS[2 * k + lax.div(c, 2), 2 * lax.rem(c, 2) + i] for i in range(2)], axis=1
+                        )
+                        for k in (2 * t, 2 * t + 1)
+                    ],
+                    axis=0,
+                )
+                u, base = lax.div(c, 2), 2 * lax.rem(c, 2)
+                right = jnp.concatenate([G[0, u, base + i, t * HT : (t + 1) * HT] for i in range(2)], axis=1)
+            else:
+                at = slice(t * HT, (t + 1) * HT)
+                left = jnp.concatenate([R[m - 1, own, c, at], I[m - 1, c, at]], axis=1)
+                right = jnp.concatenate([G[m, own, c, at], J[m - 1, c, at]], axis=1)
+            lh, ll = split(left)
+            rh, rl = split(right)
+            total = dot3(lh, ll, rh, rl, 0, 0)
             table = TT[m]
             for i in range(2):
                 hi, lo = split(total[i * 128 : (i + 1) * 128])
@@ -415,12 +390,37 @@
                 for j in range(2):
                     jj = j if m == 0 else lax.rem(own + j, 2)
                     for zz in range(4):
-                        GO[m, zz, ii, c, jj] = back[zz * 32 : (zz + 1) * 32, j * 128 : (j + 1) * 128]
+                        piece = back[zz * 32 : (zz + 1) * 32, j * 128 : (j + 1) * 128]
+                        GO[m, zz, ii, c, jj] = piece if t == 0 else GO[m, zz, ii, c, jj] + piece
             return carry
 
         lax.fori_loop(0, 4, one, 0)
+        if t == 1 and m == 0:
+            for zz in range(4):
+                x_first(zz).start()
+        if t == 1 and m > 0:
+            for d in (1, 3, 2):
+                z_send(m, d).start()
+
+    def x_land(zz):
+        return XG.at[0] if zz == 3 else GL.at[0, zz, 1]
+
+    def x_first(zz):
+        return remote(
+            GO.at[0, zz, 1 - xlo], x_land(zz), zs.at[4, zz], zr.at[4, zz], xlo_peer
+        )
+
+    def z_last(d):
+        return remote(
+            GO.at[0, lax.rem(z + d, 4), xlo], GL.at[0, d - 1, 0], zs.at[0, d - 1], zr.at[0, d - 1], z_peer(d)
+        )
+
+    def x_sum():
+        for zz in range(4):
+            x_first(zz).wait_recv()
+            GO[0, zz, xlo] = GO[0, zz, xlo] + x_land(zz)[...]
         for d in (1, 3, 2):
-            z_send(m, d).start()
+            z_last(d).start()
 
     def z_send(m, d):
         return remote(
@@ -437,27 +437,21 @@
             GO[m, z, side] = GO[m, z, side] + GL[m, 0, side] + GL[m, 1, side] + GL[m, 2, side]
         u_send(m).start()
 
-    def adam(m):
-        u_send(m).wait_recv()
-
-        def one(c, carry):
-            for j in range(2):
-                at = slice(j * 128, (j + 1) * 128)
-                grad = GO[m, z, xlo, c, j] + XG[m, c, j]
-                moment = beta_one * AD[0, m, c, :, at] + (1.0 - beta_one) * grad
-                second = beta_two * AD[1, m, c, :, at] + (1.0 - beta_two) * grad * grad
-                step = learn_rate * (moment / bias_one) / (jnp.sqrt(second / bias_two) + epsilon)
-                AD[0, m, c, :, at] = moment
-                AD[1, m, c, :, at] = second
-                AD[2, m, c, :, at] = AD[2, m, c, :, at] - step
-            return carry
-
-        lax.fori_loop(0, 4, one, 0)
-        for i, out in enumerate((nm, ns, nb)):
-            result(m, i, out).start()
-
-    def result(m, i, out):
-        return local_copy(AD.at[i, m], out.at[m], osem.at[i, m])
+    def share_sum(m):
+        if m == 0:
+            for d in (1, 3, 2):
+                z_last(d).wait_recv()
+            GO[0, z, xlo] = GO[0, z, xlo] + GL[0, 0, 0] + GL[0, 1, 0] + GL[0, 2, 0]
+        else:
+            u_send(m).wait_recv()
+            GO[m, z, xlo] = GO[m, z, xlo] + XG[m]
+        result(m).start()
+
+    def result(m):
+        return local_copy(GO.at[m, z, xlo], go.at[m], osem.at[m])
+
+    def kv_result():
+        return local_copy(KV, kvo, osem.at[4])
 
     def p_core(k):
         return remote(
@@ -530,10 +524,10 @@
         at = slice(k * CT, (k + 1) * CT)
         key_tile = jnp.where(core == 0, FT[k], KP[at])
         value_tile = jnp.where(core == 0, KP[at], FT[k])
-        key_tile = jnp.where(core == 0, key_tile, pltpu.roll(key_tile, 64, 1))
-        value_tile = jnp.where(core == 0, value_tile, pltpu.roll(value_tile, 64, 1))
-        ko[at, :] = key_tile[:, :64]
-        vo[at, :] = value_tile[:, :64]
+        key_tile = jnp.transpose(key_tile)
+        value_tile = jnp.transpose(value_tile)
+        KV[:64, at] = jnp.where(core == 0, key_tile[:64], key_tile[64:])
+        KV[64:, at] = jnp.where(core == 0, value_tile[:64], value_tile[64:])
 
     def fwd_last(k):
         bwd_back(3, k).wait_send()
@@ -547,76 +541,83 @@
         fwd_back(1, k).wait_send()
         bwd_step(1, k)
 
-    bwd_next(2, 0)
-    bwd_next(2, 1)
-    bwd_mid(0)
-    bwd_next(2, 2)
-    bwd_mid(1)
-    bwd_next(2, 3)
-    bwd_mid(2)
-    fwd_last(0)
-    for h in range(2):
-        gx(h).wait_send()
-        gc(h).wait_send()
-        for far in range(2):
-            for d in (1, 3, 2):
-                gy(d, h, far).wait_send()
-    bwd_next(1, 0)
-    bwd_mid(3)
-    fwd_last(1)
-    bwd_low(0)
-    bwd_next(1, 1)
-    fwd_last(2)
-    bwd_low(1)
-    bwd_next(1, 2)
-    fwd_last(3)
-    bwd_low(2)
-    gradient(3)
-    gradient(2)
-    pair_copy.wait_send()
-    fwd_back(3, 0).wait_recv()
-    project(0)
-    bwd_next(1, 3)
-    project_y(0)
-    bwd_low(3)
-    fwd_back(3, 1).wait_recv()
-    project(1)
+    def gather_done():
+        for h in range(2):
+            gx(h).wait_send()
+            gc(h).wait_send()
+            for far in range(2):
+                for d in (1, 3, 2):
+                    gy(d, h, far).wait_send()
+
+    def bwd_low_out(k):
+        if k == 0:
+            gather_done()
+        bwd_next(1, k)
+
+    def bwd_grad0(t):
+        for k in (2 * t, 2 * t + 1):
+            bwd_back(1, k).wait_recv()
+            for cp in x_again[k]:
+                cp.wait()
+        gradient(0, t)
+
+    def project_in(k):
+        fwd_back(3, k).wait_recv()
+        project(k)
+
+    def late_prepare(m):
+        prepare(m, m % 2, third_blocks if m == 2 else fourth_blocks)
+        if m == 3:
+            for group in x_again:
+                for cp in group:
+                    cp.start()
+
+    steps_of = {
+        "Q": late_prepare,
+        "T": tiles,
+        "X": gather_far,
+        "TY": gather_near,
+        "Z": gathered,
+        "W": weights,
+        "H": upstream,
+        "HS": lambda k: bwd_out(3, k).start(),
+        "B": fwd_first,
+        "C": lambda k: fwd_next(2, k),
+        "D": lambda k: fwd_step(2, k),
+        "E": lambda k: fwd_next(3, k),
+        "F": fwd_last,
+        "I": lambda k: bwd_step(3, k),
+        "J": lambda k: bwd_next(2, k),
+        "K": bwd_mid,
+        "L": bwd_low_out,
+        "M": bwd_low,
+        "G": gradient,
+        "N": bwd_grad0,
+        "P": project_in,
+        "PY": project_y,
+        "PX": project_x,
+        "PL": project_last,
+        "PO": project_out,
+        "S": z_sum,
+        "SX": x_sum,
+        "U": share_sum,
+    }
+
+    tiles_send()
     for k in range(NC):
-        bwd_back(1, k).wait_recv()
-    gradient(1)
-    for group in x_again:
-        for cp in group:
-            cp.wait()
-    gradient(0)
-    project_y(1)
-    project_x(0)
-    project_last(0)
-    for cp in adam_loads:
-        cp.wait()
-    project_x(1)
-    project_last(1)
-    fwd_back(3, 2).wait_recv()
-    project(2)
-    fwd_back(3, 3).wait_recv()
-    project_y(2)
-    z_sum(3)
-    project(3)
-    z_sum(2)
-    project_y(3)
-    project_out(0)
-    project_out(1)
-    adam(3)
-    adam(2)
-    z_sum(1)
-    project_x(2)
-    project_last(2)
-    z_sum(0)
-    project_x(3)
-    project_last(3)
-    adam(1)
-    adam(0)
-    project_out(2)
-    project_out(3)
+        first_factor(k)
+    prepare(1, 1, second_blocks)
+    fourth_blocks = block_loads(3, 1)
+    for cp in fourth_blocks:
+        cp.start()
+    pl.semaphore_wait(barrier, len(peers))
+    pair_copy.start()
+    for k in range(NC):
+        fwd_out(1, k).start()
+
+    for name, *args in ORDER:
+        steps_of[name](*args)
+    kv_result().start()
 
     for m in (1, 2, 3):
         for k in range(NC):
@@ -632,16 +633,70 @@
         for d in (1, 3, 2):
             p_y(k, d).wait_send()
         p_x(k).wait_send()
+    pair_copy.wait_send()
     for m in range(4):
         for d in (1, 3, 2):
-            z_send(m, d).wait_send()
-        u_send(m).wait_send()
-        for i, out in enumerate((nm, ns, nb)):
-            result(m, i, out).wait()
+            (z_send(m, d) if m else z_last(d)).wait_send()
+        if m:
+            u_send(m).wait_send()
+        result(m).wait()
+    for zz in range(4):
+        x_first(zz).wait_send()
+    kv_result().wait()
+
+
+def finish(g, kv, mo, se, bl, ko, vo, nb, nm, ns, GV, KB, A, isem, jsem, osem):
+    tok = lax.axis_index("tok")
+    share = pl.ds(pl.multiple_of(tok * 32, 32), 32)
+    copy = pltpu.make_async_copy
+
+    def loads(m):
+        return [
+            copy(g.at[m], GV.at[m], isem.at[0, m]),
+            copy(mo.at[m], A.at[0, m], isem.at[1, m]),
+            copy(se.at[m], A.at[1, m], isem.at[2, m]),
+            copy(bl.at[m, :, share, :], A.at[2, m], isem.at[3, m]),
+        ]
+
+    def stores(m):
+        return [copy(A.at[i, m], out.at[m], osem.at[i, m]) for i, out in enumerate((nm, ns, nb))]
+
+    kv_load = copy(kv, KB, jsem.at[0])
+    kv_load.start()
+    every = [loads(m) for m in range(4)]
+    for group in every:
+        for cp in group:
+            cp.start()
+    kv_load.wait()
+    kv_stores = [
+        copy(KB.at[pl.ds(0, 64)], ko, jsem.at[1]),
+        copy(KB.at[pl.ds(64, 64)], vo, jsem.at[2]),
+    ]
+    for cp in kv_stores:
+        cp.start()
+    for m in range(4):
+        for cp in every[m]:
+            cp.wait()
+        for c in range(4):
+            for j in range(2):
+                at = slice(j * 128, (j + 1) * 128)
+                grad = GV[m, c, j]
+                moment = beta_one * A[0, m, c, :, at] + (1.0 - beta_one) * grad
+                second = beta_two * A[1, m, c, :, at] + (1.0 - beta_two) * grad * grad
+                step = learn_rate * (moment / bias_one) / (jnp.sqrt(second / bias_two) + epsilon)
+                A[0, m, c, :, at] = moment
+                A[1, m, c, :, at] = second
+                A[2, m, c, :, at] = A[2, m, c, :, at] - step
+        for cp in stores(m):
+            cp.start()
+    for m in range(4):
+        for cp in stores(m):
+            cp.wait()
+    for cp in kv_stores:
+        cp.wait()
 
 
 def local(x, kw, vw, bl, ro, kg, vg, mo, se):
-    kv = jnp.concatenate([kg, vg], axis=1)
     hbm = pl.BlockSpec(memory_space=pl.ANY)
     vmem = pl.BlockSpec(memory_space=pltpu.VMEM)
     dma = pltpu.SemaphoreType.DMA
@@ -654,7 +709,7 @@
         pltpu.VMEM((4, 4, 256, 256), BF16),
         pltpu.VMEM((4,) + tile, BF16),
         pltpu.VMEM((4,) + tile, BF16),
-        pltpu.VMEM((2, 128, 1024), F32),
+        pltpu.VMEM((4, 128, 1024), F32),
         pltpu.VMEM((8, 4) + tile, F32),
         pltpu.VMEM((4, 2, 4, 512, 128), F32),
         pltpu.VMEM((3, 4, 512, 128), F32),
@@ -672,13 +727,12 @@
         pltpu.VMEM((4, 4, 2, 4, 2, 32, 128), F32),
         pltpu.VMEM((4, 3, 2, 4, 2, 32, 128), F32),
         pltpu.VMEM((4, 4, 2, 32, 128), F32),
-        pltpu.VMEM((3, 4, 4, 32, 256), F32),
+        pltpu.VMEM((128, 512), F32),
         dma((4, 4)),
         dma((2, 4, 8)),
+        dma((4,)),
         dma((2,)),
-        dma(()),
-        dma((3,)),
-        dma((3, 4)),
+        dma((5,)),
         dma((2, 3, 2, 4)),
         dma((2, 3, 2, 4)),
         dma((5,)),
@@ -687,23 +741,41 @@
         dma((2, 3, 2)),
         dma((6, 4)),
         dma((6, 4)),
-        dma((4, 3)),
-        dma((4, 3)),
+        dma((5, 4)),
+        dma((5, 4)),
         dma((4,)),
         dma((4,)),
     ]
     share = jax.ShapeDtypeStruct((4, 4, 32, 256), F32)
-    narrow = jax.ShapeDtypeStruct((512, 64), F32)
-    return pl.pallas_call(
+    narrow = jax.ShapeDtypeStruct((64, 512), F32)
+    grads, kv = pl.pallas_call(
         kernel,
-        out_shape=(narrow, narrow, share, share, share),
-        in_specs=[hbm, hbm, hbm, hbm, vmem, hbm, hbm, hbm],
-        out_specs=(vmem, vmem, hbm, hbm, hbm),
+        out_shape=(
+            jax.ShapeDtypeStruct((4, 4, 2, 32, 128), F32),
+            jax.ShapeDtypeStruct((128, 512), F32),
+        ),
+        in_specs=[hbm, hbm, hbm, hbm, vmem, hbm, hbm],
+        out_specs=(hbm, hbm),
         scratch_shapes=scratch,
         compiler_params=pltpu.CompilerParams(
             collective_id=0, has_side_effects=True, vmem_limit_bytes=67043328
         ),
-    )(x, kw, vw, bl, ro, kv, mo, se)
+    )(x, kw, vw, bl, ro, kg.T, vg.T)
+    ko, vo, nb, nm, ns = pl.pallas_call(
+        finish,
+        out_shape=(narrow, narrow, share, share, share),
+        in_specs=[hbm] * 5,
+        out_specs=(hbm,) * 5,
+        scratch_shapes=[
+            pltpu.VMEM((4, 4, 2, 32, 128), F32),
+            pltpu.VMEM((128, 512), F32),
+            pltpu.VMEM((3, 4, 4, 32, 256), F32),
+            dma((4, 4)),
+            dma((3,)),
+            dma((3, 4)),
+        ],
+    )(grads, kv, mo, se, bl)
+    return ko.T, vo.T, nb, nm, ns
 
 
 def solution(mesh):

time: 189 us -> 174 us (0.921)
  local copies, waits for them, and re-layouts: 11.1 us -> 0 us
  Pallas kernels: 175 us -> 173 us
    unnamed x5 -> x0, local copies, waits for them, and re-layouts: 7.7 us -> none
    pallas_call x2 -> x0, local copies, waits for them, and re-layouts: 3.44 us -> none  [local(): pl.pallas_call(kernel, out_shape=(narrow, narrow, share, share, share), i...]
    pallas_call x1 -> x2, Pallas kernels: 175 us -> 173 us  [the longest x1 170 us: local(): pl.pallas_call(kernel, out_shape=(jax.ShapeDtypeStruct((4, 4, 2, 32, 128)...]
where the time goes in v1:
time: 174 us; the launch traced here: 173 us
  Pallas kernels  173 us (99%)
    pallas_call x1, Pallas kernels, local(): pl.pallas_call(kernel, out_shape=(jax.ShapeDtypeStruct((4, 4, 2, 32, 128)...  170 us

profile of v1, /device:TPU:1, one launch (start us, length us, event | category | flops | bytes accessed | tf_op | source)
XLA Modules:
  0.0 173.5 jit_solution(16602789558085498906)
XLA Ops:
  0.6 169.5 %shard_map.128 = (f32[4,4,2,32,128]{4,3,2,1,0:T(8,128)}, f32[128,512]{1,0:T(8,128)}) custom-call(f32[512,1024]{1,0:T(8,128)} %x.1, f32[1024,1024]{1,0:T(8,128)} %kw.1, f32[1024,1024]{1,0:T(8,128)} %vw.1, f32[4,4,256,256]{3,2,1,0:T(8,128)} %bl.3, s32[4,128]{1,0:T(4,128)} %ro.1, f32[64,512]{1,0:T(8,128)} %bitcast.4, f32[64,512]{1,0:T(8,128)} %bitcast.5), custom_call_target="tpu_custom_call" | custom-call | tf_op jit(solution)/shard_map/pallas_call | solution.py:751
  170.2 3.2 %shard_map.129 = (f32[64,512]{1,0:T(8,128)}, f32[64,512]{1,0:T(8,128)}, f32[4,4,32,256]{3,2,1,0:T(8,128)}, f32[4,4,32,256]{3,2,1,0:T(8,128)}, f32[4,4,32,256]{3,2,1,0:T(8,128)}) custom-call(f32[4,4,2,32,128]{4,3,2,1,0:T(8,128)} %get-tuple-element.12.g, f32[128,512]{1,0:T(8,128)} %get-tuple-element.13.kv, f32[4,4,32,256]{3,2,1,0:T(8,128)} %mo.1, ...), custom_call_target="tpu_custom_call" | custom-call | tf_op jit(solution)/shard_map/pallas_call | solution.py:764

commit v2 on v1

--- a/solution.py
+++ b/solution.py
@@ -16,18 +16,17 @@
 bias_two = 1.0 - 0.95**10
 
 ORDER = (
-    ("W", 0), ("W", 1), ("T",), ("TY", 0), ("B", 1), ("B", 2), ("B", 0), ("C", 1), ("B", 3),
-    ("W", 2), ("W", 3), ("C", 0), ("C", 3), ("X", 0), ("TY", 1), ("Q", 2), ("W", 4), ("W", 5),
-    ("D", 1), ("Z", 0), ("W", 6), ("W", 7), ("X", 1), ("H", 0), ("HS", 0), ("Q", 3), ("Z", 1),
-    ("HS", 1), ("D", 3), ("D", 0), ("I", 0), ("H", 1), ("I", 1), ("C", 2), ("HS", 3), ("J", 0),
-    ("HS", 2), ("J", 1), ("K", 0), ("I", 3), ("K", 1), ("I", 2), ("G", 2, 0), ("L", 0), ("E", 1),
-    ("E", 0), ("J", 3), ("M", 0), ("L", 1), ("J", 2), ("M", 1), ("G", 1, 0), ("K", 3), ("F", 1),
-    ("D", 2), ("N", 0), ("K", 2), ("F", 0), ("E", 3), ("G", 2, 1), ("G", 3, 0), ("L", 3), ("P", 1),
-    ("M", 3), ("PY", 1), ("P", 0), ("E", 2), ("L", 2), ("PY", 0), ("F", 3), ("S", 2), ("M", 2),
-    ("G", 1, 1), ("N", 1), ("PX", 1), ("U", 2), ("F", 2), ("G", 3, 1), ("PX", 0), ("S", 1),
-    ("SX",), ("PL", 1), ("P", 3), ("U", 1), ("PY", 3), ("PL", 0), ("P", 2), ("S", 3), ("PO", 1),
-    ("PO", 0), ("PY", 2), ("U", 0), ("PX", 3), ("U", 3), ("PL", 3), ("PX", 2), ("PO", 3),
-    ("PL", 2), ("PO", 2),
+    ("Q", 2), ("T",), ("TY", 0), ("W", 0), ("W", 1), ("B", 3), ("B", 1), ("B", 0), ("W", 2),
+    ("W", 3), ("C", 3), ("X", 0), ("W", 4), ("X", 1), ("C", 0), ("Q", 3), ("C", 1), ("W", 5),
+    ("D", 3), ("TY", 1), ("W", 6), ("W", 7), ("Z", 0), ("H", 0), ("HS", 0), ("B", 2), ("D", 0),
+    ("C", 2), ("Z", 1), ("D", 1), ("HS", 1), ("I", 0), ("H", 1), ("I", 1), ("J", 0), ("HS", 3),
+    ("J", 1), ("HS", 2), ("K", 0), ("I", 3), ("K", 1), ("I", 2), ("L", 0), ("J", 3), ("E", 1),
+    ("M", 0), ("G", 2, 0), ("E", 0), ("L", 1), ("J", 2), ("M", 1), ("G", 1, 0), ("K", 3), ("F", 1),
+    ("N", 0), ("D", 2), ("K", 2), ("F", 0), ("G", 2, 1), ("E", 3), ("L", 3), ("P", 1), ("M", 3),
+    ("E", 2), ("PY", 1), ("P", 0), ("L", 2), ("PY", 0), ("F", 3), ("M", 2), ("S", 2), ("G", 1, 1),
+    ("PX", 1), ("N", 1), ("F", 2), ("G", 3, 0), ("PX", 0), ("G", 3, 1), ("U", 2), ("PL", 1),
+    ("P", 3), ("PO", 1), ("PY", 3), ("S", 1), ("PL", 0), ("P", 2), ("SX", 0), ("PY", 2), ("S", 3),
+    ("U", 1), ("U", 0), ("PO", 0), ("PL", 2), ("PL", 3), ("PO", 3), ("PO", 2), ("U", 3),
 )
 
 CT = 128
@@ -55,7 +54,7 @@
 def kernel(
     x, kw, vw, bl, ro, kg, vg,
     go, kvo,
-    XP, WH, WL, AH, AL, TT, TS, ST, BS, R, I, T, G, J, GKV, KT, KP, LH, LL, YL, XL, FT, GO, GL, XG, KV,
+    XP, WH, WL, AH, AL, TT, TS, ST, BS, R, I, T, G, J, GKV, KT, KP, LH, LL, YL, XL, DL, FT, GO, GL, XG, KV,
     bsem, xsem, stsem, ktsem, osem,
     ss, rs, kvs, kvr, gs, gr, ps, pr, zs, zr, us, ur,
 ):
@@ -68,7 +67,7 @@
     y = lax.div(feat, 4)
     yhi = lax.div(feat, 8)
     yx = lax.rem(feat, 4)
-    chip = lax.div(feat, 2)
+    chip = xhi * 4 + y
     bits = [None, core, xhi, yhi]
     steps = [None, 1, 2, 8]
 
@@ -79,6 +78,9 @@
 
     def y_peer(d):
         return (tok, lax.rem(y + d, 4) * 4 + yx)
+
+    def xy_peer(d):
+        return (tok, lax.rem(y + d, 4) * 4 + yx + 2 - 4 * xhi)
 
     def z_peer(d):
         return (xlo * 4 + lax.rem(z + d, 4), feat)
@@ -148,6 +150,7 @@
 
     barrier = pltpu.get_barrier_semaphore()
     peers = [core_peer, x_peer, y_peer(1), y_peer(2), y_peer(3), z_peer(1), z_peer(2), z_peer(3), xlo_peer]
+    peers += [xy_peer(1), xy_peer(2), xy_peer(3)]
     for dev in peers:
         pl.semaphore_signal(barrier, inc=1, device_id=dev, device_id_type=MESH)
 
@@ -242,7 +245,7 @@
         lax.fori_loop(0, 4, one, 0)
 
     pair_copy = remote(KT, KP, kvs.at[0], kvr.at[0], core_peer)
-    chip_x = chip + 1 - 2 * xhi
+    chip_x = (1 - xhi) * 4 + y
 
     def gx(h):
         return remote(
@@ -320,8 +323,9 @@
         for s in range(2):
             for t in range(8):
                 hi, lo = split(GKV[s, t, h * HT : (h + 1) * HT, :])
-                LH[s, :, t * 128 : (t + 1) * 128] = hi
-                LL[s, :, t * 128 : (t + 1) * 128] = lo
+                col = (t % 4) * 2 + t // 4
+                LH[s, :, col * 128 : (col + 1) * 128] = hi
+                LL[s, :, col * 128 : (col + 1) * 128] = lo
         for u in range(2):
 
             def one(n, carry, u=u):
@@ -415,7 +419,7 @@
             GO.at[0, lax.rem(z + d, 4), xlo], GL.at[0, d - 1, 0], zs.at[0, d - 1], zr.at[0, d - 1], z_peer(d)
         )
 
-    def x_sum():
+    def x_sum(m):
         for zz in range(4):
             x_first(zz).wait_recv()
             GO[0, zz, xlo] = GO[0, zz, xlo] + x_land(zz)[...]
@@ -450,24 +454,36 @@
     def result(m):
         return local_copy(GO.at[m, z, xlo], go.at[m], osem.at[m])
 
-    def kv_result():
-        return local_copy(KV, kvo, osem.at[4])
+    def kv_result(k):
+        return local_copy(KV.at[:, rows(k)], kvo.at[:, rows(k)], osem.at[4 + k])
 
     def p_core(k):
         return remote(
             XP.at[k % 2, 1 - core], GKV.at[0, :, rows(k)], ps.at[0, k], pr.at[0, k], core_peer
         )
 
+    def p_x(k):
+        return remote(
+            XP.at[k % 2, core, pl.ds(4 * (1 - xhi), 4)], XL.at[k], ps.at[4, k], pr.at[4, k], x_peer
+        )
+
     def p_y(k, d):
-        yy = lax.rem(y + d, 4)
-        return remote(
-            XP.at[k % 2, core, pl.ds(2 * yy, 2)], YL.at[d - 1, k], ps.at[d, k], pr.at[d, k], y_peer(d)
-        )
-
-    def p_x(k):
-        return remote(
-            XP.at[k % 2, core, 2 * y + 1 - xhi], XL.at[k], ps.at[4, k], pr.at[4, k], x_peer
-        )
+        return remote(
+            XP.at[k % 2, core, 4 * xhi + lax.rem(y + d, 4)], YL.at[d - 1, k], ps.at[d, k], pr.at[d, k], y_peer(d)
+        )
+
+    def p_all(k):
+        found = []
+        for slot, d, other in ((4, 1, 1), (6, 3, 1), (5, 2, 1), (3, 0, 1), (0, 1, 0), (2, 3, 0), (1, 2, 0)):
+            side = 1 - xhi if other else xhi
+            dev = (x_peer if d == 0 else xy_peer(d)) if other else y_peer(d)
+            found.append(
+                remote(
+                    XP.at[k % 2, core, 4 * side + lax.rem(y + d, 4)], DL.at[slot, k - 2],
+                    ps.at[6 + slot, k], pr.at[6 + slot, k], dev,
+                )
+            )
+        return found
 
     def p_last(k):
         return remote(FT.at[k], KP.at[rows(k)], ps.at[5, k], pr.at[5, k], core_peer)
@@ -488,8 +504,8 @@
 
             def one(n, carry, s=s):
                 out = dot3(LH[0, :CT, :], LL[0, :CT, :], WH[s, n], WL[s, n])
-                XP[k % 2, s, 2 * n] = out[:, :128]
-                XP[k % 2, s, 2 * n + 1] = out[:, 128:]
+                XP[k % 2, s, n] = out[:, :128]
+                XP[k % 2, s, 4 + n] = out[:, 128:]
                 return carry
 
             lax.fori_loop(0, 4, one, 0)
@@ -503,20 +519,32 @@
             return carry
 
         lax.fori_loop(0, 8, one, 0)
+        if k < 2:
+            p_x(k).start()
+        else:
+            for cp in p_all(k):
+                cp.start()
+
+    def project_x(k):
+        p_x(k).wait_recv()
+        for t in range(4):
+            XP[k % 2, core, 4 * xhi + t] = XP[k % 2, core, 4 * xhi + t] + XL[k, t]
         for d in (1, 3, 2):
             p_y(k, d).start()
 
-    def project_x(k):
-        for d in (1, 3, 2):
-            p_y(k, d).wait_recv()
-        for side in (1 - xhi, xhi):
-            at = 2 * y + side
-            XP[k % 2, core, at] = XP[k % 2, core, at] + YL[0, k, side] + YL[1, k, side] + YL[2, k, side]
-        p_x(k).start()
-
     def project_last(k):
-        p_x(k).wait_recv()
-        FT[k] = XP[k % 2, core, 2 * y + xhi] + XL[k]
+        total = None
+        if k < 2:
+            for d in (1, 3, 2):
+                p_y(k, d).wait_recv()
+            total = XP[k % 2, core, chip] + YL[0, k] + YL[1, k] + YL[2, k]
+        else:
+            for cp in p_all(k):
+                cp.wait_recv()
+            total = XP[k % 2, core, chip]
+            for slot in range(7):
+                total = total + DL[slot, k - 2]
+        FT[k] = total
         p_last(k).start()
 
     def project_out(k):
@@ -528,6 +556,7 @@
         value_tile = jnp.transpose(value_tile)
         KV[:64, at] = jnp.where(core == 0, key_tile[:64], key_tile[64:])
         KV[64:, at] = jnp.where(core == 0, value_tile[:64], value_tile[64:])
+        kv_result(k).start()
 
     def fwd_last(k):
         bwd_back(3, k).wait_send()
@@ -617,7 +646,6 @@
 
     for name, *args in ORDER:
         steps_of[name](*args)
-    kv_result().start()
 
     for m in (1, 2, 3):
         for k in range(NC):
@@ -630,9 +658,8 @@
         p_last(k).wait_send()
     for k in (2, 3):
         p_core(k).wait_send()
-        for d in (1, 3, 2):
-            p_y(k, d).wait_send()
-        p_x(k).wait_send()
+        for cp in p_all(k):
+            cp.wait_send()
     pair_copy.wait_send()
     for m in range(4):
         for d in (1, 3, 2):
@@ -642,7 +669,8 @@
         result(m).wait()
     for zz in range(4):
         x_first(zz).wait_send()
-    kv_result().wait()
+    for k in range(NC):
+        kv_result(k).wait()
 
 
 def finish(g, kv, mo, se, bl, ko, vo, nb, nm, ns, GV, KB, A, isem, jsem, osem):
@@ -721,8 +749,9 @@
         pltpu.VMEM((512, 128), F32),
         pltpu.VMEM((2, 256, 1024), BF16),
         pltpu.VMEM((2, 256, 1024), BF16),
-        pltpu.VMEM((3, 4, 2) + tile, F32),
-        pltpu.VMEM((4,) + tile, F32),
+        pltpu.VMEM((3, 2) + tile, F32),
+        pltpu.VMEM((2, 4) + tile, F32),
+        pltpu.VMEM((7, 2) + tile, F32),
         pltpu.VMEM((4,) + tile, F32),
         pltpu.VMEM((4, 4, 2, 4, 2, 32, 128), F32),
         pltpu.VMEM((4, 3, 2, 4, 2, 32, 128), F32),
@@ -732,15 +761,15 @@
         dma((2, 4, 8)),
         dma((4,)),
         dma((2,)),
-        dma((5,)),
+        dma((8,)),
         dma((2, 3, 2, 4)),
         dma((2, 3, 2, 4)),
         dma((5,)),
         dma((5,)),
         dma((2, 3, 2)),
         dma((2, 3, 2)),
-        dma((6, 4)),
-        dma((6, 4)),
+        dma((13, 4)),
+        dma((13, 4)),
         dma((5, 4)),
         dma((5, 4)),
         dma((4,)),

time: 174 us -> 166 us (0.954); the launches traced: 173 us -> 163 us
  Pallas kernels: 173 us -> 163 us
    pallas_call x1, Pallas kernels: 170 us -> 159 us  [local(): pl.pallas_call(kernel, out_shape=(jax.ShapeDtypeStruct((4, 4, 2, 32, 128)...]
where the time goes in v2:
time: 166 us; the launch traced here: 163 us
  Pallas kernels  163 us (98%)
    pallas_call x1, Pallas kernels, local(): pl.pallas_call(kernel, out_shape=(jax.ShapeDtypeStruct((4, 4, 2, 32, 128)...  159 us

profile of v2, /device:TPU:1, one launch (start us, length us, event | category | flops | bytes accessed | tf_op | source)
XLA Modules:
  0.0 163.3 jit_solution(8969673757956168962)
XLA Ops:
  0.6 159.4 %shard_map.128 = (f32[4,4,2,32,128]{4,3,2,1,0:T(8,128)}, f32[128,512]{1,0:T(8,128)}) custom-call(f32[512,1024]{1,0:T(8,128)} %x.1, f32[1024,1024]{1,0:T(8,128)} %kw.1, f32[1024,1024]{1,0:T(8,128)} %vw.1, f32[4,4,256,256]{3,2,1,0:T(8,128)} %bl.3, s32[4,128]{1,0:T(4,128)} %ro.1, f32[64,512]{1,0:T(8,128)} %bitcast.4, f32[64,512]{1,0:T(8,128)} %bitcast.5), custom_call_target="tpu_custom_call" | custom-call | tf_op jit(solution)/shard_map/pallas_call | solution.py:780
  160.0 3.2 %shard_map.129 = (f32[64,512]{1,0:T(8,128)}, f32[64,512]{1,0:T(8,128)}, f32[4,4,32,256]{3,2,1,0:T(8,128)}, f32[4,4,32,256]{3,2,1,0:T(8,128)}, f32[4,4,32,256]{3,2,1,0:T(8,128)}) custom-call(f32[4,4,2,32,128]{4,3,2,1,0:T(8,128)} %get-tuple-element.12.g, f32[128,512]{1,0:T(8,128)} %get-tuple-element.13.kv, f32[4,4,32,256]{3,2,1,0:T(8,128)} %mo.1, ...), custom_call_target="tpu_custom_call" | custom-call | tf_op jit(solution)/shard_map/pallas_call | solution.py:793

commit v3 on v2

--- a/solution.py
+++ b/solution.py
@@ -16,17 +16,17 @@
 bias_two = 1.0 - 0.95**10
 
 ORDER = (
-    ("Q", 2), ("T",), ("TY", 0), ("W", 0), ("W", 1), ("B", 3), ("B", 1), ("B", 0), ("W", 2),
-    ("W", 3), ("C", 3), ("X", 0), ("W", 4), ("X", 1), ("C", 0), ("Q", 3), ("C", 1), ("W", 5),
-    ("D", 3), ("TY", 1), ("W", 6), ("W", 7), ("Z", 0), ("H", 0), ("HS", 0), ("B", 2), ("D", 0),
-    ("C", 2), ("Z", 1), ("D", 1), ("HS", 1), ("I", 0), ("H", 1), ("I", 1), ("J", 0), ("HS", 3),
-    ("J", 1), ("HS", 2), ("K", 0), ("I", 3), ("K", 1), ("I", 2), ("L", 0), ("J", 3), ("E", 1),
-    ("M", 0), ("G", 2, 0), ("E", 0), ("L", 1), ("J", 2), ("M", 1), ("G", 1, 0), ("K", 3), ("F", 1),
-    ("N", 0), ("D", 2), ("K", 2), ("F", 0), ("G", 2, 1), ("E", 3), ("L", 3), ("P", 1), ("M", 3),
-    ("E", 2), ("PY", 1), ("P", 0), ("L", 2), ("PY", 0), ("F", 3), ("M", 2), ("S", 2), ("G", 1, 1),
-    ("PX", 1), ("N", 1), ("F", 2), ("G", 3, 0), ("PX", 0), ("G", 3, 1), ("U", 2), ("PL", 1),
-    ("P", 3), ("PO", 1), ("PY", 3), ("S", 1), ("PL", 0), ("P", 2), ("SX", 0), ("PY", 2), ("S", 3),
-    ("U", 1), ("U", 0), ("PO", 0), ("PL", 2), ("PL", 3), ("PO", 3), ("PO", 2), ("U", 3),
+    ("T",), ("Q", 1), ("W", 0), ("TY", 0), ("B", 3), ("B", 1), ("C", 3), ("B", 0), ("W", 1),
+    ("X", 0), ("W", 2), ("X", 1), ("Q", 2), ("B", 2), ("W", 3), ("C", 0), ("C", 1), ("C", 2),
+    ("TY", 1), ("W", 4), ("D", 3), ("W", 5), ("W", 6), ("Z", 0), ("W", 7), ("H", 0), ("HS", 0),
+    ("Q", 3), ("D", 0), ("Z", 1), ("HS", 1), ("D", 1), ("I", 0), ("H", 1), ("I", 1), ("J", 0),
+    ("HS", 3), ("J", 1), ("HS", 2), ("K", 0), ("I", 3), ("K", 1), ("I", 2), ("G", 2, 0), ("E", 1),
+    ("E", 0), ("L", 0), ("J", 3), ("M", 0), ("L", 1), ("J", 2), ("M", 1), ("G", 1, 0), ("K", 3),
+    ("F", 1), ("D", 2), ("N", 0), ("K", 2), ("F", 0), ("G", 2, 1), ("E", 3), ("L", 3), ("P", 1),
+    ("M", 3), ("E", 2), ("PY", 1), ("P", 0), ("L", 2), ("PY", 0), ("F", 3), ("M", 2), ("S", 2),
+    ("G", 1, 1), ("PX", 1), ("N", 1), ("F", 2), ("G", 3, 0), ("PX", 0), ("G", 3, 1), ("U", 2),
+    ("PL", 1), ("P", 3), ("PY", 3), ("S", 1), ("PL", 0), ("P", 2), ("SX", 0), ("PO", 1), ("PY", 2),
+    ("PL", 3), ("S", 3), ("U", 1), ("PO", 0), ("PO", 3), ("U", 0), ("PL", 2), ("PO", 2), ("U", 3),
 )
 
 CT = 128
@@ -177,11 +177,6 @@
 
         lax.fori_loop(0, 4, one, 0)
 
-    prepare(0, 0, first_blocks)
-    third_blocks = block_loads(2, 0)
-    for cp in third_blocks:
-        cp.start()
-
     def fwd_out(m, k):
         return remote(
             R.at[m - 1, 1 - bits[m], :, rows(k)], I.at[m - 1, :, rows(k)],
@@ -202,7 +197,7 @@
 
     def bwd_back(m, k):
         return remote(
-            T.at[m - 1, :, rows(k)], G.at[m - 1, bits[m], :, rows(k)],
+            T.at[3 if m == 2 else m - 1, :, rows(k)], G.at[m - 1, bits[m], :, rows(k)],
             ss.at[1, m - 1, 1, k], rs.at[1, m - 1, 1, k], flip(m),
         )
 
@@ -239,7 +234,7 @@
             hi, lo = split(pair)
             out = dot3(hi, lo, AH[m, c], AL[m, c], 1, 1)
             G[m - 1, own, c, rows(k)] = out[:, :128]
-            T[m - 1, c, rows(k)] = out[:, 128:]
+            T[3 if m == 2 else m - 1, c, rows(k)] = out[:, 128:]
             return carry
 
         lax.fori_loop(0, 4, one, 0)
@@ -563,7 +558,6 @@
         fwd_step(3, k)
 
     def bwd_mid(k):
-        fwd_back(2, k).wait_send()
         bwd_step(2, k)
 
     def bwd_low(k):
@@ -595,7 +589,10 @@
         project(k)
 
     def late_prepare(m):
-        prepare(m, m % 2, third_blocks if m == 2 else fourth_blocks)
+        prepare(m, m % 2, {1: second_blocks, 2: third_blocks, 3: fourth_blocks}[m])
+        if m == 1:
+            for cp in fourth_blocks:
+                cp.start()
         if m == 3:
             for group in x_again:
                 for cp in group:
@@ -633,15 +630,15 @@
     }
 
     tiles_send()
-    for k in range(NC):
-        first_factor(k)
-    prepare(1, 1, second_blocks)
+    prepare(0, 0, first_blocks)
+    third_blocks = block_loads(2, 0)
+    for cp in third_blocks:
+        cp.start()
     fourth_blocks = block_loads(3, 1)
-    for cp in fourth_blocks:
-        cp.start()
     pl.semaphore_wait(barrier, len(peers))
     pair_copy.start()
     for k in range(NC):
+        first_factor(k)
         fwd_out(1, k).start()
 
     for name, *args in ORDER:
@@ -653,6 +650,7 @@
             bwd_out(m, k).wait_send()
     for k in range(NC):
         fwd_back(3, k).wait_send()
+        fwd_back(2, k).wait_send()
         bwd_back(2, k).wait_send()
         bwd_back(1, k).wait_send()
         p_last(k).wait_send()
@@ -741,7 +739,7 @@
         pltpu.VMEM((8, 4) + tile, F32),
         pltpu.VMEM((4, 2, 4, 512, 128), F32),
         pltpu.VMEM((3, 4, 512, 128), F32),
-        pltpu.VMEM((3, 4, 512, 128), F32),
+        pltpu.VMEM((4, 4, 512, 128), F32),
         pltpu.VMEM((4, 2, 4, 512, 128), F32),
         pltpu.VMEM((3, 4, 512, 128), F32),
         pltpu.VMEM((2, 8, 512, 128), F32),

time: 166 us -> 159 us (0.958); the launches traced: 163 us -> 159 us
  Pallas kernels: 163 us -> 158 us
    pallas_call x1, Pallas kernels: 159 us -> 155 us  [local(): pl.pallas_call(kernel, out_shape=(jax.ShapeDtypeStruct((4, 4, 2, 32, 128)...]
where the time goes in v3:
time: 159 us
  Pallas kernels  158 us (99%)
    pallas_call x1, Pallas kernels, local(): pl.pallas_call(kernel, out_shape=(jax.ShapeDtypeStruct((4, 4, 2, 32, 128)...  155 us

profile of v3, /device:TPU:1, one launch (start us, length us, event | category | flops | bytes accessed | tf_op | source)
XLA Modules:
  0.0 158.7 jit_solution(12768621549686580807)
XLA Ops:
  0.6 154.7 %shard_map.128 = (f32[4,4,2,32,128]{4,3,2,1,0:T(8,128)}, f32[128,512]{1,0:T(8,128)}) custom-call(f32[512,1024]{1,0:T(8,128)} %x.1, f32[1024,1024]{1,0:T(8,128)} %kw.1, f32[1024,1024]{1,0:T(8,128)} %vw.1, f32[4,4,256,256]{3,2,1,0:T(8,128)} %bl.3, s32[4,128]{1,0:T(4,128)} %ro.1, f32[64,512]{1,0:T(8,128)} %bitcast.4, f32[64,512]{1,0:T(8,128)} %bitcast.5), custom_call_target="tpu_custom_call" | custom-call | tf_op jit(solution)/shard_map/pallas_call | solution.py:778
  155.3 3.2 %shard_map.129 = (f32[64,512]{1,0:T(8,128)}, f32[64,512]{1,0:T(8,128)}, f32[4,4,32,256]{3,2,1,0:T(8,128)}, f32[4,4,32,256]{3,2,1,0:T(8,128)}, f32[4,4,32,256]{3,2,1,0:T(8,128)}) custom-call(f32[4,4,2,32,128]{4,3,2,1,0:T(8,128)} %get-tuple-element.12.g, f32[128,512]{1,0:T(8,128)} %get-tuple-element.13.kv, f32[4,4,32,256]{3,2,1,0:T(8,128)} %mo.1, ...), custom_call_target="tpu_custom_call" | custom-call | tf_op jit(solution)/shard_map/pallas_call | solution.py:791

commit v4 on v3

--- a/solution.py
+++ b/solution.py
@@ -16,17 +16,17 @@
 bias_two = 1.0 - 0.95**10
 
 ORDER = (
-    ("T",), ("Q", 1), ("W", 0), ("TY", 0), ("B", 3), ("B", 1), ("C", 3), ("B", 0), ("W", 1),
-    ("X", 0), ("W", 2), ("X", 1), ("Q", 2), ("B", 2), ("W", 3), ("C", 0), ("C", 1), ("C", 2),
-    ("TY", 1), ("W", 4), ("D", 3), ("W", 5), ("W", 6), ("Z", 0), ("W", 7), ("H", 0), ("HS", 0),
-    ("Q", 3), ("D", 0), ("Z", 1), ("HS", 1), ("D", 1), ("I", 0), ("H", 1), ("I", 1), ("J", 0),
-    ("HS", 3), ("J", 1), ("HS", 2), ("K", 0), ("I", 3), ("K", 1), ("I", 2), ("G", 2, 0), ("E", 1),
-    ("E", 0), ("L", 0), ("J", 3), ("M", 0), ("L", 1), ("J", 2), ("M", 1), ("G", 1, 0), ("K", 3),
-    ("F", 1), ("D", 2), ("N", 0), ("K", 2), ("F", 0), ("G", 2, 1), ("E", 3), ("L", 3), ("P", 1),
-    ("M", 3), ("E", 2), ("PY", 1), ("P", 0), ("L", 2), ("PY", 0), ("F", 3), ("M", 2), ("S", 2),
-    ("G", 1, 1), ("PX", 1), ("N", 1), ("F", 2), ("G", 3, 0), ("PX", 0), ("G", 3, 1), ("U", 2),
-    ("PL", 1), ("P", 3), ("PY", 3), ("S", 1), ("PL", 0), ("P", 2), ("SX", 0), ("PO", 1), ("PY", 2),
-    ("PL", 3), ("S", 3), ("U", 1), ("PO", 0), ("PO", 3), ("U", 0), ("PL", 2), ("PO", 2), ("U", 3),
+    ("W", 0), ("W", 1), ("T",), ("TY", 0), ("B", 2), ("W", 2), ("Q", 2), ("W", 3), ("B", 0),
+    ("C", 2), ("X", 0), ("Q", 3), ("TY", 1), ("C", 0), ("B", 1), ("B", 3), ("W", 4), ("W", 5),
+    ("Z", 0), ("C", 3), ("C", 1), ("X", 1), ("W", 6), ("W", 7), ("H", 0), ("HS", 0), ("D", 0),
+    ("HS", 1), ("D", 1), ("Z", 1), ("I", 0), ("D", 3), ("I", 1), ("H", 1), ("HS", 3), ("HS", 2),
+    ("J", 0), ("J", 1), ("K", 0), ("I", 3), ("K", 1), ("I", 2), ("L", 0), ("J", 3), ("M", 0),
+    ("E", 1), ("G", 2, 0), ("E", 0), ("L", 1), ("J", 2), ("M", 1), ("G", 1, 0), ("K", 3), ("F", 1),
+    ("N", 0), ("D", 2), ("K", 2), ("F", 0), ("G", 2, 1), ("G", 3, 0), ("L", 3), ("E", 3), ("P", 1),
+    ("M", 3), ("PY", 1), ("E", 2), ("P", 0), ("L", 2), ("PY", 0), ("F", 3), ("M", 2), ("S", 2),
+    ("G", 1, 1), ("PX", 1), ("F", 2), ("N", 1), ("PX", 0), ("G", 3, 1), ("U", 2), ("PL", 1),
+    ("P", 3), ("PY", 3), ("S", 1), ("PL", 0), ("P", 2), ("SX", 0), ("PY", 2), ("S", 3), ("U", 1),
+    ("PL", 3), ("U", 0), ("PL", 2), ("PO", 2), ("PO", 3), ("PO", 0), ("PO", 1), ("U", 3),
 )
 
 CT = 128
@@ -55,7 +55,7 @@
     x, kw, vw, bl, ro, kg, vg,
     go, kvo,
     XP, WH, WL, AH, AL, TT, TS, ST, BS, R, I, T, G, J, GKV, KT, KP, LH, LL, YL, XL, DL, FT, GO, GL, XG, KV,
-    bsem, xsem, stsem, ktsem, osem,
+    bsem, xsem, xbsem, stsem, ktsem, osem,
     ss, rs, kvs, kvr, gs, gr, ps, pr, zs, zr, us, ur,
 ):
     tok = lax.axis_index("tok")
@@ -111,14 +111,14 @@
                     local_copy(
                         bl.at[m, :, pl.ds(r0, 128), pl.ds(c0, 128)],
                         BS.at[pl.ds(4 * slot, 4), 2 * i + j],
-                        bsem.at[m, 2 * i + j],
+                        bsem.at[m],
                     )
                 )
         return copies
 
-    def x_loads(k, to, at, sem):
+    def x_loads(k, to, sem_of):
         return [
-            local_copy(x.at[pl.ds(k * CT, CT), pl.ds(h * 128, 128)], to(k, h), xsem.at[sem, k, h])
+            local_copy(x.at[pl.ds(k * CT, CT), pl.ds(h * 128, 128)], to(k, h), sem_of(k, h))
             for h in range(8)
         ]
 
@@ -131,7 +131,7 @@
     first_blocks = block_loads(0, 0)
     for cp in first_blocks:
         cp.start()
-    x_copies = [x_loads(k, lambda k, h: XP.at[k // 2, k % 2, h], None, 0) for k in range(NC)]
+    x_copies = [x_loads(k, lambda k, h: XP.at[k // 2, k % 2, h], lambda k, h: xsem.at[k, h]) for k in range(NC)]
     for cp in x_copies[0]:
         cp.start()
     second_blocks = block_loads(1, 1)
@@ -160,9 +160,10 @@
         TT[m] = hot.astype(BF16)
         TS[m] = jnp.transpose(hot).astype(BF16)
 
-    def prepare(m, slot, copies):
-        for cp in copies:
-            cp.wait()
+    corner = pl.ds(0, 128)
+
+    def prepare(m, slot):
+        local_copy(bl.at[:, :, corner, corner], BS.at[pl.ds(4 * slot, 4)], bsem.at[m]).wait()
         table = TS[m]
 
         def one(c, carry):
@@ -252,8 +253,12 @@
         tile = chip_x if far else chip
         return remote(
             GKV.at[core, tile, rows(h, HT)], GKV.at[core, tile, rows(h, HT)],
-            gs.at[far, d - 1, h], gr.at[far, d - 1, h], y_peer(d),
-        )
+            gs.at[far, h], gr.at[far, h], y_peer(d),
+        )
+
+    def gy_three(h, far):
+        three = GKV.at[core, pl.ds(0, 3), rows(h, HT)]
+        return remote(three, three, gs.at[far, h], gr.at[far, h], y_peer(1))
 
     def gc(h):
         return remote(
@@ -305,12 +310,11 @@
             if step + 4 < 16:
                 w_load(step + 4).start()
 
-    x_again = [x_loads(k, lambda k, h: BS.at[2 * k + h // 4, h % 4], None, 1) for k in range(NC)]
+    x_again = [x_loads(k, lambda k, h: BS.at[2 * k + h // 4, h % 4], lambda k, h: xbsem.at[k]) for k in range(NC)]
 
     def gathered(h):
         for far in range(2):
-            for d in (1, 3, 2):
-                gy(d, h, far).wait_recv()
+            gy_three(h, far).wait_recv()
         gc(h).start()
 
     def upstream(h):
@@ -406,40 +410,46 @@
 
     def x_first(zz):
         return remote(
-            GO.at[0, zz, 1 - xlo], x_land(zz), zs.at[4, zz], zr.at[4, zz], xlo_peer
+            GO.at[0, zz, 1 - xlo], x_land(zz), zs.at[4], zr.at[4], xlo_peer
         )
 
     def z_last(d):
         return remote(
-            GO.at[0, lax.rem(z + d, 4), xlo], GL.at[0, d - 1, 0], zs.at[0, d - 1], zr.at[0, d - 1], z_peer(d)
+            GO.at[0, lax.rem(z + d, 4), xlo], GL.at[0, d - 1, 0], zs.at[0], zr.at[0], z_peer(d)
         )
 
     def x_sum(m):
+        x_four().wait_recv()
         for zz in range(4):
-            x_first(zz).wait_recv()
             GO[0, zz, xlo] = GO[0, zz, xlo] + x_land(zz)[...]
         for d in (1, 3, 2):
             z_last(d).start()
 
     def z_send(m, d):
         return remote(
-            GO.at[m, lax.rem(z + d, 4)], GL.at[m, d - 1], zs.at[m, d - 1], zr.at[m, d - 1], z_peer(d)
-        )
+            GO.at[m, lax.rem(z + d, 4)], GL.at[m, d - 1], zs.at[m], zr.at[m], z_peer(d)
+        )
+
+    def z_three(m):
+        land = GL.at[m] if m else GL.at[0, :, 0]
+        return remote(land, land, zs.at[m], zr.at[m], z_peer(1))
+
+    def x_four():
+        land = GO.at[0, :, xlo]
+        return remote(land, land, zs.at[4], zr.at[4], xlo_peer)
 
     def u_send(m):
         return remote(GO.at[m, z, 1 - xlo], XG.at[m], us.at[m], ur.at[m], xlo_peer)
 
     def z_sum(m):
-        for d in (1, 3, 2):
-            z_send(m, d).wait_recv()
+        z_three(m).wait_recv()
         for side in (1 - xlo, xlo):
             GO[m, z, side] = GO[m, z, side] + GL[m, 0, side] + GL[m, 1, side] + GL[m, 2, side]
         u_send(m).start()
 
     def share_sum(m):
         if m == 0:
-            for d in (1, 3, 2):
-                z_last(d).wait_recv()
+            z_three(0).wait_recv()
             GO[0, z, xlo] = GO[0, z, xlo] + GL[0, 0, 0] + GL[0, 1, 0] + GL[0, 2, 0]
         else:
             u_send(m).wait_recv()
@@ -454,17 +464,17 @@
 
     def p_core(k):
         return remote(
-            XP.at[k % 2, 1 - core], GKV.at[0, :, rows(k)], ps.at[0, k], pr.at[0, k], core_peer
+            XP.at[k % 2, 1 - core], GKV.at[0, :, rows(k)], ps.at[k], pr.at[k], core_peer
         )
 
     def p_x(k):
         return remote(
-            XP.at[k % 2, core, pl.ds(4 * (1 - xhi), 4)], XL.at[k], ps.at[4, k], pr.at[4, k], x_peer
+            XP.at[k % 2, core, pl.ds(4 * (1 - xhi), 4)], XL.at[k], ps.at[8 + k], pr.at[8 + k], x_peer
         )
 
     def p_y(k, d):
         return remote(
-            XP.at[k % 2, core, 4 * xhi + lax.rem(y + d, 4)], YL.at[d - 1, k], ps.at[d, k], pr.at[d, k], y_peer(d)
+            XP.at[k % 2, core, 4 * xhi + lax.rem(y + d, 4)], YL.at[d - 1, k], ps.at[10 + k], pr.at[10 + k], y_peer(d)
         )
 
     def p_all(k):
@@ -475,19 +485,22 @@
             found.append(
                 remote(
                     XP.at[k % 2, core, 4 * side + lax.rem(y + d, 4)], DL.at[slot, k - 2],
-                    ps.at[6 + slot, k], pr.at[6 + slot, k], dev,
+                    ps.at[10 + k], pr.at[10 + k], dev,
                 )
             )
         return found
 
+    def p_group(k):
+        land = YL.at[:, k] if k < 2 else DL.at[:, k - 2]
+        return remote(land, land, ps.at[10 + k], pr.at[10 + k], y_peer(1))
+
     def p_last(k):
-        return remote(FT.at[k], KP.at[rows(k)], ps.at[5, k], pr.at[5, k], core_peer)
+        return remote(FT.at[k], KP.at[rows(k)], ps.at[4 + k], pr.at[4 + k], core_peer)
 
     def project(k):
         if k >= 2:
             p_core(k - 2).wait_send()
-            for d in (1, 3, 2):
-                p_y(k - 2, d).wait_send()
+            p_group(k - 2).wait_send()
             p_x(k - 2).wait_send()
         for u in range(2):
             for c in range(4):
@@ -530,12 +543,10 @@
     def project_last(k):
         total = None
         if k < 2:
-            for d in (1, 3, 2):
-                p_y(k, d).wait_recv()
+            p_group(k).wait_recv()
             total = XP[k % 2, core, chip] + YL[0, k] + YL[1, k] + YL[2, k]
         else:
-            for cp in p_all(k):
-                cp.wait_recv()
+            p_group(k).wait_recv()
             total = XP[k % 2, core, chip]
             for slot in range(7):
                 total = total + DL[slot, k - 2]
@@ -569,8 +580,7 @@
             gx(h).wait_send()
             gc(h).wait_send()
             for far in range(2):
-                for d in (1, 3, 2):
-                    gy(d, h, far).wait_send()
+                gy_three(h, far).wait_send()
 
     def bwd_low_out(k):
         if k == 0:
@@ -580,8 +590,9 @@
     def bwd_grad0(t):
         for k in (2 * t, 2 * t + 1):
             bwd_back(1, k).wait_recv()
-            for cp in x_again[k]:
-                cp.wait()
+            local_copy(
+                bl.at[pl.ds(0, 2), :, corner, corner], BS.at[pl.ds(2 * k, 2)], xbsem.at[k]
+            ).wait()
         gradient(0, t)
 
     def project_in(k):
@@ -589,10 +600,7 @@
         project(k)
 
     def late_prepare(m):
-        prepare(m, m % 2, {1: second_blocks, 2: third_blocks, 3: fourth_blocks}[m])
-        if m == 1:
-            for cp in fourth_blocks:
-                cp.start()
+        prepare(m, m % 2)
         if m == 3:
             for group in x_again:
                 for cp in group:
@@ -630,45 +638,49 @@
     }
 
     tiles_send()
-    prepare(0, 0, first_blocks)
+    prepare(0, 0)
     third_blocks = block_loads(2, 0)
     for cp in third_blocks:
         cp.start()
+    for k in range(NC):
+        first_factor(k)
+    prepare(1, 1)
     fourth_blocks = block_loads(3, 1)
+    for cp in fourth_blocks:
+        cp.start()
     pl.semaphore_wait(barrier, len(peers))
     pair_copy.start()
     for k in range(NC):
-        first_factor(k)
         fwd_out(1, k).start()
 
     for name, *args in ORDER:
         steps_of[name](*args)
 
-    for m in (1, 2, 3):
+    def sends_end():
+        for m in (1, 2, 3):
+            for k in range(NC):
+                fwd_out(m, k).wait_send()
+                bwd_out(m, k).wait_send()
         for k in range(NC):
-            fwd_out(m, k).wait_send()
-            bwd_out(m, k).wait_send()
-    for k in range(NC):
-        fwd_back(3, k).wait_send()
-        fwd_back(2, k).wait_send()
-        bwd_back(2, k).wait_send()
-        bwd_back(1, k).wait_send()
-        p_last(k).wait_send()
-    for k in (2, 3):
-        p_core(k).wait_send()
-        for cp in p_all(k):
-            cp.wait_send()
-    pair_copy.wait_send()
-    for m in range(4):
-        for d in (1, 3, 2):
-            (z_send(m, d) if m else z_last(d)).wait_send()
-        if m:
-            u_send(m).wait_send()
-        result(m).wait()
-    for zz in range(4):
-        x_first(zz).wait_send()
-    for k in range(NC):
-        kv_result(k).wait()
+            fwd_back(3, k).wait_send()
+            fwd_back(2, k).wait_send()
+            bwd_back(2, k).wait_send()
+            bwd_back(1, k).wait_send()
+            p_last(k).wait_send()
+        for k in (2, 3):
+            p_core(k).wait_send()
+            p_group(k).wait_send()
+        pair_copy.wait_send()
+        for m in range(4):
+            z_three(m).wait_send()
+            if m:
+                u_send(m).wait_send()
+            result(m).wait()
+        x_four().wait_send()
+        for k in range(NC):
+            kv_result(k).wait()
+
+    sends_end()
 
 
 def finish(g, kv, mo, se, bl, ko, vo, nb, nm, ns, GV, KB, A, isem, jsem, osem):
@@ -755,8 +767,9 @@
         pltpu.VMEM((4, 3, 2, 4, 2, 32, 128), F32),
         pltpu.VMEM((4, 4, 2, 32, 128), F32),
         pltpu.VMEM((128, 512), F32),
-        dma((4, 4)),
-        dma((2, 4, 8)),
+        dma((4,)),
+        dma((4, 8)),
+        dma((4,)),
         dma((4,)),
         dma((2,)),
         dma((8,)),
@@ -764,12 +777,12 @@
         dma((2, 3, 2, 4)),
         dma((5,)),
         dma((5,)),
-        dma((2, 3, 2)),
-        dma((2, 3, 2)),
-        dma((13, 4)),
-        dma((13, 4)),
-        dma((5, 4)),
-        dma((5, 4)),
+        dma((2, 2)),
+        dma((2, 2)),
+        dma((14,)),
+        dma((14,)),
+        dma((5,)),
+        dma((5,)),
         dma((4,)),
         dma((4,)),
     ]

time: 159 us -> 157 us (0.987)
  Pallas kernels: 158 us -> 156 us
    pallas_call x1, Pallas kernels: 155 us -> 152 us  [local(): pl.pallas_call(kernel, out_shape=(jax.ShapeDtypeStruct((4, 4, 2, 32, 128)...]
where the time goes in v4:
time: 157 us; the launch traced here: 156 us
  Pallas kernels  156 us (99%)
    pallas_call x1, Pallas kernels, local(): pl.pallas_call(kernel, out_shape=(jax.ShapeDtypeStruct((4, 4, 2, 32, 128)...  152 us
    pallas_call x1, Pallas kernels, local(): pl.pallas_call(finish, out_shape=(narrow, narrow, share, share, share), i...  3.16 us

profile of v4, /device:TPU:1, one launch (start us, length us, event | category | flops | bytes accessed | tf_op | source)
XLA Modules:
  0.0 156.4 jit_solution(15050869183809442409)
XLA Ops:
  0.6 152.4 %shard_map.128 = (f32[4,4,2,32,128]{4,3,2,1,0:T(8,128)}, f32[128,512]{1,0:T(8,128)}) custom-call(f32[512,1024]{1,0:T(8,128)} %x.1, f32[1024,1024]{1,0:T(8,128)} %kw.1, f32[1024,1024]{1,0:T(8,128)} %vw.1, f32[4,4,256,256]{3,2,1,0:T(8,128)} %bl.3, s32[4,128]{1,0:T(4,128)} %ro.1, f32[64,512]{1,0:T(8,128)} %bitcast.4, f32[64,512]{1,0:T(8,128)} %bitcast.5), custom_call_target="tpu_custom_call" | custom-call | tf_op jit(solution)/shard_map/pallas_call | solution.py:791
  153.0 3.2 %shard_map.129 = (f32[64,512]{1,0:T(8,128)}, f32[64,512]{1,0:T(8,128)}, f32[4,4,32,256]{3,2,1,0:T(8,128)}, f32[4,4,32,256]{3,2,1,0:T(8,128)}, f32[4,4,32,256]{3,2,1,0:T(8,128)}) custom-call(f32[4,4,2,32,128]{4,3,2,1,0:T(8,128)} %get-tuple-element.12.g, f32[128,512]{1,0:T(8,128)} %get-tuple-element.13.kv, f32[4,4,32,256]{3,2,1,0:T(8,128)} %mo.1, ...), custom_call_target="tpu_custom_call" | custom-call | tf_op jit(solution)/shard_map/pallas_call | solution.py:804

commit v5 on v4

--- a/solution.py
+++ b/solution.py
@@ -16,17 +16,17 @@
 bias_two = 1.0 - 0.95**10
 
 ORDER = (
-    ("W", 0), ("W", 1), ("T",), ("TY", 0), ("B", 2), ("W", 2), ("Q", 2), ("W", 3), ("B", 0),
-    ("C", 2), ("X", 0), ("Q", 3), ("TY", 1), ("C", 0), ("B", 1), ("B", 3), ("W", 4), ("W", 5),
-    ("Z", 0), ("C", 3), ("C", 1), ("X", 1), ("W", 6), ("W", 7), ("H", 0), ("HS", 0), ("D", 0),
-    ("HS", 1), ("D", 1), ("Z", 1), ("I", 0), ("D", 3), ("I", 1), ("H", 1), ("HS", 3), ("HS", 2),
-    ("J", 0), ("J", 1), ("K", 0), ("I", 3), ("K", 1), ("I", 2), ("L", 0), ("J", 3), ("M", 0),
-    ("E", 1), ("G", 2, 0), ("E", 0), ("L", 1), ("J", 2), ("M", 1), ("G", 1, 0), ("K", 3), ("F", 1),
-    ("N", 0), ("D", 2), ("K", 2), ("F", 0), ("G", 2, 1), ("G", 3, 0), ("L", 3), ("E", 3), ("P", 1),
-    ("M", 3), ("PY", 1), ("E", 2), ("P", 0), ("L", 2), ("PY", 0), ("F", 3), ("M", 2), ("S", 2),
-    ("G", 1, 1), ("PX", 1), ("F", 2), ("N", 1), ("PX", 0), ("G", 3, 1), ("U", 2), ("PL", 1),
-    ("P", 3), ("PY", 3), ("S", 1), ("PL", 0), ("P", 2), ("SX", 0), ("PY", 2), ("S", 3), ("U", 1),
-    ("PL", 3), ("U", 0), ("PL", 2), ("PO", 2), ("PO", 3), ("PO", 0), ("PO", 1), ("U", 3),
+    ("W", 0), ("T",), ("TY", 0), ("B", 2), ("B", 0), ("Q", 2), ("C", 0), ("X", 0), ("Q", 3),
+    ("B", 1), ("W", 1), ("B", 3), ("W", 2), ("W", 3), ("C", 2), ("C", 1), ("X", 1), ("W", 4),
+    ("W", 5), ("Z", 0), ("D", 0), ("W", 6), ("W", 7), ("TY", 1), ("H", 0), ("HS", 0), ("D", 2),
+    ("Z", 1), ("HS", 1), ("D", 1), ("C", 3), ("I", 0), ("I", 1), ("H", 1), ("J", 0), ("HS", 2),
+    ("HS", 3), ("J", 1), ("K", 0), ("I", 2), ("K", 1), ("I", 3), ("L", 0), ("J", 2), ("E", 0),
+    ("M", 0), ("E", 1), ("G", 2, 0), ("L", 1), ("J", 3), ("M", 1), ("G", 1, 0), ("K", 2), ("F", 0),
+    ("D", 3), ("N", 0), ("K", 3), ("F", 1), ("E", 2), ("G", 2, 1), ("L", 2), ("P", 0), ("M", 2),
+    ("PY", 0), ("E", 3), ("P", 1), ("L", 3), ("PY", 1), ("F", 2), ("M", 3), ("S", 2), ("G", 1, 1),
+    ("PX", 0), ("F", 3), ("N", 1), ("PX", 1), ("G", 3, 0), ("U", 2), ("G", 3, 1), ("PL", 0),
+    ("P", 2), ("PO", 0), ("S", 1), ("PY", 2), ("PL", 1), ("P", 3), ("SX", 0), ("U", 1), ("PY", 3),
+    ("S", 3), ("PL", 2), ("U", 0), ("PO", 1), ("PL", 3), ("U", 3), ("PO", 2), ("PO", 3),
 )
 
 CT = 128
@@ -181,26 +181,36 @@
     def fwd_out(m, k):
         return remote(
             R.at[m - 1, 1 - bits[m], :, rows(k)], I.at[m - 1, :, rows(k)],
-            ss.at[0, m - 1, 0, k], rs.at[0, m - 1, 0, k], flip(m),
+            ss.at[0, m - 1, 0], rs.at[0, m - 1, 0, k], flip(m),
         )
 
     def fwd_back(m, k):
         return remote(
             T.at[m - 1, :, rows(k)], R.at[m, bits[m], :, rows(k)],
-            ss.at[0, m - 1, 1, k], rs.at[0, m - 1, 1, k], flip(m),
+            ss.at[0, m - 1, 1], rs.at[0, m - 1, 1, k], flip(m),
         )
 
     def bwd_out(m, k):
         return remote(
             G.at[m, 1 - bits[m], :, rows(k)], J.at[m - 1, :, rows(k)],
-            ss.at[1, m - 1, 0, k], rs.at[1, m - 1, 0, k], flip(m),
+            ss.at[1, m - 1, 0], rs.at[1, m - 1, 0, k], flip(m),
         )
 
     def bwd_back(m, k):
         return remote(
             T.at[3 if m == 2 else m - 1, :, rows(k)], G.at[m - 1, bits[m], :, rows(k)],
-            ss.at[1, m - 1, 1, k], rs.at[1, m - 1, 1, k], flip(m),
-        )
+            ss.at[1, m - 1, 1], rs.at[1, m - 1, 1, k], flip(m),
+        )
+
+    def all_sent(way, m, back):
+        return remote(I.at[m - 1], I.at[m - 1], ss.at[way, m - 1, back], rs.at[way, m - 1, back, 0], flip(m))
+
+    sent = []
+
+    def wait_all_sent(way, m, back):
+        if (way, m, back) not in sent:
+            sent.append((way, m, back))
+            all_sent(way, m, back).wait_send()
 
     def first_factor(k):
         for cp in x_copies[k]:
@@ -565,14 +575,14 @@
         kv_result(k).start()
 
     def fwd_last(k):
-        bwd_back(3, k).wait_send()
+        wait_all_sent(1, 3, 1)
         fwd_step(3, k)
 
     def bwd_mid(k):
         bwd_step(2, k)
 
     def bwd_low(k):
-        fwd_back(1, k).wait_send()
+        wait_all_sent(0, 1, 1)
         bwd_step(1, k)
 
     def gather_done():
@@ -658,14 +668,10 @@
 
     def sends_end():
         for m in (1, 2, 3):
-            for k in range(NC):
-                fwd_out(m, k).wait_send()
-                bwd_out(m, k).wait_send()
+            for way in range(2):
+                for back in range(2):
+                    wait_all_sent(way, m, back)
         for k in range(NC):
-            fwd_back(3, k).wait_send()
-            fwd_back(2, k).wait_send()
-            bwd_back(2, k).wait_send()
-            bwd_back(1, k).wait_send()
             p_last(k).wait_send()
         for k in (2, 3):
             p_core(k).wait_send()
@@ -773,7 +779,7 @@
         dma((4,)),
         dma((2,)),
         dma((8,)),
-        dma((2, 3, 2, 4)),
+        dma((2, 3, 2)),
         dma((2, 3, 2, 4)),
         dma((5,)),
         dma((5,)),

time: 157 us -> 156 us (level)
  no operation moved by 1% of the time
where the time goes in v5:
time: 156 us
  Pallas kernels  155 us (99%)
    pallas_call x1, Pallas kernels, local(): pl.pallas_call(kernel, out_shape=(jax.ShapeDtypeStruct((4, 4, 2, 32, 128)...  152 us
    pallas_call x1, Pallas kernels, local(): pl.pallas_call(finish, out_shape=(narrow, narrow, share, share, share), i...  3.16 us

profile of v5, /device:TPU:1, one launch (start us, length us, event | category | flops | bytes accessed | tf_op | source)
XLA Modules:
  0.0 155.7 jit_solution(4602329892545276208)
XLA Ops:
  0.6 151.7 %shard_map.128 = (f32[4,4,2,32,128]{4,3,2,1,0:T(8,128)}, f32[128,512]{1,0:T(8,128)}) custom-call(f32[512,1024]{1,0:T(8,128)} %x.1, f32[1024,1024]{1,0:T(8,128)} %kw.1, f32[1024,1024]{1,0:T(8,128)} %vw.1, f32[4,4,256,256]{3,2,1,0:T(8,128)} %bl.3, s32[4,128]{1,0:T(4,128)} %ro.1, f32[64,512]{1,0:T(8,128)} %bitcast.4, f32[64,512]{1,0:T(8,128)} %bitcast.5), custom_call_target="tpu_custom_call" | custom-call | tf_op jit(solution)/shard_map/pallas_call | solution.py:797
  152.3 3.2 %shard_map.129 = (f32[64,512]{1,0:T(8,128)}, f32[64,512]{1,0:T(8,128)}, f32[4,4,32,256]{3,2,1,0:T(8,128)}, f32[4,4,32,256]{3,2,1,0:T(8,128)}, f32[4,4,32,256]{3,2,1,0:T(8,128)}) custom-call(f32[4,4,2,32,128]{4,3,2,1,0:T(8,128)} %get-tuple-element.12.g, f32[128,512]{1,0:T(8,128)} %get-tuple-element.13.kv, f32[4,4,32,256]{3,2,1,0:T(8,128)} %mo.1, ...), custom_call_target="tpu_custom_call" | custom-call | tf_op jit(solution)/shard_map/pallas_call | solution.py:810
